TPU v7x, 32 devices: a 4x4x1 block of a 4x4x8 slice. The times are simulated.
32 devices in a mesh: dp: 1 (over z), cp: 32 (over y, x, core).
Axes of the slice: x: 4, y: 4, z: 1, core: 2. Of those that a mesh axis runs over, the one named last changes fastest.
The devices are a block of a 4x4x8 slice.
Arguments:
- q_raw: bfloat16 [4096, 64, 128], P(('dp', 'cp'))
- k_raw: bfloat16 [4096, 8, 128], P(('dp', 'cp'))
- v_proj: bfloat16 [4096, 8, 128], P(('dp', 'cp'))
- out_fwd: bfloat16 [4096, 64, 128], P(('dp', 'cp'))
- lse_fwd: float32 [4096, 64], P(('dp', 'cp'))
- d_out: bfloat16 [4096, 64, 128], P(('dp', 'cp'))
- q_norm: float32 [128], replicated
- k_norm: float32 [128], replicated
Outputs:
- output 1: bfloat16 [4096, 64, 128], P(('dp', 'cp'))
- output 2: bfloat16 [4096, 8, 128], P(('dp', 'cp'))
- output 3: bfloat16 [4096, 8, 128], P(('dp', 'cp'))
- output 4: float32 [128], P('dp')
- output 5: float32 [128], P('dp')
All inputs are finite; a program needn't handle non-finite values.
Results may differ from a plain program's by a relative error of at most 0.00271805.
Values are sent between devices in bfloat16 or wider.
A program may use at most 768 MiB of HBM per device.

v0:
```python
import jax
import jax.numpy as jnp
from jax import lax
from jax.sharding import PartitionSpec as P

HEAD_DIM = 128
ROPE_THETA = 1000000.0
NORM_EPS = 1e-6


def rope_tables(positions):
    inv_freq = ROPE_THETA ** (-jnp.arange(0, HEAD_DIM, 2).astype(jnp.float32) / HEAD_DIM)
    angles = positions.astype(jnp.float32)[:, None] * inv_freq[None, :]
    angles = jnp.concatenate([angles, angles], axis=-1)
    return jnp.cos(angles)[:, None, :], jnp.sin(angles)[:, None, :]


def norm_rope(raw_in, weight, cos_t, sin_t):
    mean_sq = jnp.mean(raw_in * raw_in, axis=-1, keepdims=True)
    normed = raw_in * lax.rsqrt(mean_sq + NORM_EPS) * weight
    half_dim = raw_in.shape[-1] // 2
    rotated = jnp.concatenate([-normed[..., half_dim:], normed[..., :half_dim]], axis=-1)
    return normed * cos_t + rotated * sin_t


def pair_grads(q_blk, do_blk, lse_blk, delta_blk, k_blk, v_blk, visible):
    sm_scale = HEAD_DIM ** -0.5
    logits = jnp.einsum('qngd,knd->qngk', q_blk, k_blk, preferred_element_type=jnp.float32) * sm_scale - lse_blk[..., None]
    if visible is not None:
        logits = jnp.where(visible[:, None, None, :], logits, -jnp.inf)
    attn_prob = jnp.exp(logits)
    attn_dprob = jnp.einsum('qngd,knd->qngk', do_blk, v_blk, preferred_element_type=jnp.float32)
    score_grad = (attn_prob * (attn_dprob - delta_blk[..., None])).astype(jnp.bfloat16)
    prob_bf = attn_prob.astype(jnp.bfloat16)
    dq_part = sm_scale * jnp.einsum('qngk,knd->qngd', score_grad, k_blk, preferred_element_type=jnp.float32)
    dk_part = sm_scale * jnp.einsum('qngk,qngd->knd', score_grad, q_blk, preferred_element_type=jnp.float32)
    dv_part = jnp.einsum('qngk,qngd->knd', prob_bf, do_blk, preferred_element_type=jnp.float32)
    return dq_part, dk_part, dv_part


def own_grads(q_b, do_b, lse_b, delta_sum, k_blk, v_blk):
    chunk_len = k_blk.shape[0] // 2
    tri_mask = jnp.arange(chunk_len)[:, None] >= jnp.arange(chunk_len)[None, :]
    dq_first, dk_first, dv_first = pair_grads(q_b[:chunk_len], do_b[:chunk_len], lse_b[:chunk_len], delta_sum[:chunk_len], k_blk[:chunk_len], v_blk[:chunk_len], tri_mask)
    dq_cross, dk_cross, dv_cross = pair_grads(q_b[chunk_len:], do_b[chunk_len:], lse_b[chunk_len:], delta_sum[chunk_len:], k_blk[:chunk_len], v_blk[:chunk_len], None)
    dq_second, dk_second, dv_second = pair_grads(q_b[chunk_len:], do_b[chunk_len:], lse_b[chunk_len:], delta_sum[chunk_len:], k_blk[chunk_len:], v_blk[chunk_len:], tri_mask)
    dq_own = jnp.concatenate([dq_first, dq_cross + dq_second])
    dk_own = jnp.concatenate([dk_first + dk_cross, dk_second])
    dv_own = jnp.concatenate([dv_first + dv_cross, dv_second])
    return dq_own, dk_own, dv_own


def early_source(q_b, do_b, lse_b, delta_sum, k_blk, v_blk, dq_acc, dk_acc, dv_acc):
    chunk_len = k_blk.shape[0] // 2
    dq_part, dk_part, dv_part = pair_grads(q_b, do_b, lse_b, delta_sum, k_blk[:chunk_len], v_blk[:chunk_len], None)
    return (dq_acc + dq_part,
            jnp.concatenate([dk_acc[:chunk_len] + dk_part, dk_acc[chunk_len:]]),
            jnp.concatenate([dv_acc[:chunk_len] + dv_part, dv_acc[chunk_len:]]))


def late_source(q_b, do_b, lse_b, delta_sum, k_blk, v_blk, dq_acc, dk_acc, dv_acc):
    chunk_len = k_blk.shape[0] // 2
    dq_part, dk_part, dv_part = pair_grads(q_b[chunk_len:], do_b[chunk_len:], lse_b[chunk_len:], delta_sum[chunk_len:], k_blk, v_blk, None)
    return (jnp.concatenate([dq_acc[:chunk_len], dq_acc[chunk_len:] + dq_part]),
            dk_acc + dk_part,
            dv_acc + dv_part)


def solution(mesh):
    cp_size = mesh.shape['cp']
    shift_pairs = [(source, (source + 1) % cp_size) for source in range(cp_size)]

    def local_grads(q_raw, k_raw, v_proj, out_fwd, lse_fwd, d_out, q_norm, k_norm):
        dev_rank = lax.axis_index('cp')
        local_rows, num_heads = q_raw.shape[0], q_raw.shape[1]
        chunk_len = local_rows // 2
        kv_heads = k_raw.shape[1]
        per_kv = num_heads // kv_heads
        offsets = jnp.arange(chunk_len)
        positions = jnp.concatenate([dev_rank * chunk_len + offsets, (2 * cp_size - 1 - dev_rank) * chunk_len + offsets])
        cos_t, sin_t = rope_tables(positions)
        prepare = lambda raw_in, weight: norm_rope(raw_in, weight, cos_t, sin_t)
        q_full, pull_q = jax.vjp(prepare, q_raw.astype(jnp.float32), q_norm)
        k_full, pull_k = jax.vjp(prepare, k_raw.astype(jnp.float32), k_norm)
        q_b = q_full.astype(jnp.bfloat16).reshape(local_rows, kv_heads, per_kv, HEAD_DIM)
        k_b = k_full.astype(jnp.bfloat16)
        do_b = d_out.reshape(local_rows, kv_heads, per_kv, HEAD_DIM)
        lse_b = lse_fwd.reshape(local_rows, kv_heads, per_kv)
        delta_sum = jnp.einsum('thd,thd->th', d_out, out_fwd, preferred_element_type=jnp.float32).reshape(local_rows, kv_heads, per_kv)
        dq_acc, dk_acc, dv_acc = own_grads(q_b, do_b, lse_b, delta_sum, k_b, v_proj)

        def visit_source(step_idx, loop_state):
            k_cur, v_cur, dq_cur, dk_cur, dv_cur = loop_state
            k_cur = lax.ppermute(k_cur, 'cp', shift_pairs)
            v_cur = lax.ppermute(v_cur, 'cp', shift_pairs)
            dk_cur = lax.ppermute(dk_cur, 'cp', shift_pairs)
            dv_cur = lax.ppermute(dv_cur, 'cp', shift_pairs)
            source = (dev_rank - step_idx) % cp_size
            dq_cur, dk_cur, dv_cur = lax.cond(source < dev_rank, early_source, late_source, q_b, do_b, lse_b, delta_sum, k_cur, v_cur, dq_cur, dk_cur, dv_cur)
            return k_cur, v_cur, dq_cur, dk_cur, dv_cur

        loop_state = lax.fori_loop(1, cp_size, visit_source, (k_b, v_proj, dq_acc, dk_acc, dv_acc))
        dq_acc, dk_cur, dv_cur = loop_state[2], loop_state[3], loop_state[4]
        dk_home = lax.ppermute(dk_cur, 'cp', shift_pairs)
        dv_home = lax.ppermute(dv_cur, 'cp', shift_pairs)
        dq_raw, dq_weight = pull_q(dq_acc.reshape(local_rows, num_heads, HEAD_DIM))
        dk_raw, dk_weight = pull_k(dk_home)
        return (dq_raw.astype(jnp.bfloat16), dk_raw.astype(jnp.bfloat16), dv_home.astype(jnp.bfloat16),
                lax.psum(dq_weight, 'cp'), lax.psum(dk_weight, 'cp'))

    row_spec = P(('dp', 'cp'))
    in_specs = (row_spec, row_spec, row_spec, row_spec, row_spec, row_spec, P(), P())
    out_specs = (row_spec, row_spec, row_spec, P('dp'), P('dp'))
    return jax.shard_map(local_grads, mesh=mesh, in_specs=in_specs, out_specs=out_specs, check_vma=False)
```

profile of v0, /device:TPU:97, one launch (start us, length us, event | category | flops | bytes accessed | tf_op | source)
XLA Modules:
  0.0 1315.8 jit_solution(10512588934146049094)
XLA Ops:
  61.2 1163.3 %while.23 = (s32[]{:T(128)}, bf16[128,8,128]{2,0,1:T(8,128)(2,1)}, bf16[128,8,128]{2,0,1:T(8,128)(2,1)}, f32[128,8,8,128]{3,0,2,1:T(8,128)}, f32[128,8,128]{2,0,...) while((s32[]{:T(128)}, bf16[128,8,128]{2,0,1:T(8,128)(2,1)}, ...), condition=%wide.region_5.6_spmd, body=%wide.region_2.5_spmd.sunk | while | flops 677838848 | bytes 84837048 | solution.py:102
  65.6 12.8 collective-permute-done.1
  81.9 10.2 conditional.2
  97.2 12.8 collective-permute-done.1
  113.5 13.4 %conditional.2 = (f32[128,8,8,128]{3,0,2,1:T(8,128)}, f32[128,8,128]{2,0,1:T(8,128)S(1)}, f32[128,8,128]{2,0,1:T(8,128)}) conditional(s32[]{:T(128)} %convert_element_type.148, (f32[128,8,8,128]{3,0,2,1:T(8,128)}, bf16[128,8,8,128]{3,0,2,1:T(8,128)(2,1)S(1)}, bf16[128,8,128]{2,0,1:T(8,128)(2,1)S(1)}, f32[128,8,8]{0,2,1:T(8,128)S(1)}, ...), branch_computations={%region_3.3_spmd, %region_4.4_spmd} | conditional | flops 677838848 | bytes 75399248 | solution.py:99
  128.8 14.1 %collective-permute-done.1 = bf16[128,8,128]{2,0,1:T(8,128)(2,1)} collective-permute-done((bf16[128,8,128]{2,0,1:T(8,128)(2,1)}, bf16[128,8,128]{2,0,1:T(8,128)(2,1)}, u32[]{:S(2)}, u32[]{:S(2)}) %collective-permute-start.1) | collective-permute-done | bytes 262176 | tf_op jit(solution)/shard_map/while/body/eval_jaxpr/ppermute | solution.py:95
  145.7 13.4 %conditional.2 = (f32[128,8,8,128]{3,0,2,1:T(8,128)}, f32[128,8,128]{2,0,1:T(8,128)S(1)}, f32[128,8,128]{2,0,1:T(8,128)}) conditional(s32[]{:T(128)} %convert_element_type.148, (f32[128,8,8,128]{3,0,2,1:T(8,128)}, bf16[128,8,8,128]{3,0,2,1:T(8,128)(2,1)S(1)}, bf16[128,8,128]{2,0,1:T(8,128)(2,1)S(1)}, f32[128,8,8]{0,2,1:T(8,128)S(1)}, ...), branch_computations={%region_3.3_spmd, %region_4.4_spmd} | conditional | flops 677838848 | bytes 75399248 | solution.py:99
  162.5 18.4 %collective-permute-done.1 = bf16[128,8,128]{2,0,1:T(8,128)(2,1)} collective-permute-done((bf16[128,8,128]{2,0,1:T(8,128)(2,1)}, bf16[128,8,128]{2,0,1:T(8,128)(2,1)}, u32[]{:S(2)}, u32[]{:S(2)}) %collective-permute-start.1) | collective-permute-done | bytes 262176 | tf_op jit(solution)/shard_map/while/body/eval_jaxpr/ppermute | solution.py:95
  183.3 13.4 %conditional.2 = (f32[128,8,8,128]{3,0,2,1:T(8,128)}, f32[128,8,128]{2,0,1:T(8,128)S(1)}, f32[128,8,128]{2,0,1:T(8,128)}) conditional(s32[]{:T(128)} %convert_element_type.148, (f32[128,8,8,128]{3,0,2,1:T(8,128)}, bf16[128,8,8,128]{3,0,2,1:T(8,128)(2,1)S(1)}, bf16[128,8,128]{2,0,1:T(8,128)(2,1)S(1)}, f32[128,8,8]{0,2,1:T(8,128)S(1)}, ...), branch_computations={%region_3.3_spmd, %region_4.4_spmd} | conditional | flops 677838848 | bytes 75399248 | solution.py:99
  197.6 21.3 %collective-permute-done.1 = bf16[128,8,128]{2,0,1:T(8,128)(2,1)} collective-permute-done((bf16[128,8,128]{2,0,1:T(8,128)(2,1)}, bf16[128,8,128]{2,0,1:T(8,128)(2,1)}, u32[]{:S(2)}, u32[]{:S(2)}) %collective-permute-start.1) | collective-permute-done | bytes 262176 | tf_op jit(solution)/shard_map/while/body/eval_jaxpr/ppermute | solution.py:95
  221.3 13.4 %conditional.2 = (f32[128,8,8,128]{3,0,2,1:T(8,128)}, f32[128,8,128]{2,0,1:T(8,128)S(1)}, f32[128,8,128]{2,0,1:T(8,128)}) conditional(s32[]{:T(128)} %convert_element_type.148, (f32[128,8,8,128]{3,0,2,1:T(8,128)}, bf16[128,8,8,128]{3,0,2,1:T(8,128)(2,1)S(1)}, bf16[128,8,128]{2,0,1:T(8,128)(2,1)S(1)}, f32[128,8,8]{0,2,1:T(8,128)S(1)}, ...), branch_computations={%region_3.3_spmd, %region_4.4_spmd} | conditional | flops 677838848 | bytes 75399248 | solution.py:99
  235.7 21.3 %collective-permute-done.1 = bf16[128,8,128]{2,0,1:T(8,128)(2,1)} collective-permute-done((bf16[128,8,128]{2,0,1:T(8,128)(2,1)}, bf16[128,8,128]{2,0,1:T(8,128)(2,1)}, u32[]{:S(2)}, u32[]{:S(2)}) %collective-permute-start.1) | collective-permute-done | bytes 262176 | tf_op jit(solution)/shard_map/while/body/eval_jaxpr/ppermute | solution.py:95
  259.4 13.4 %conditional.2 = (f32[128,8,8,128]{3,0,2,1:T(8,128)}, f32[128,8,128]{2,0,1:T(8,128)S(1)}, f32[128,8,128]{2,0,1:T(8,128)}) conditional(s32[]{:T(128)} %convert_element_type.148, (f32[128,8,8,128]{3,0,2,1:T(8,128)}, bf16[128,8,8,128]{3,0,2,1:T(8,128)(2,1)S(1)}, bf16[128,8,128]{2,0,1:T(8,128)(2,1)S(1)}, f32[128,8,8]{0,2,1:T(8,128)S(1)}, ...), branch_computations={%region_3.3_spmd, %region_4.4_spmd} | conditional | flops 677838848 | bytes 75399248 | solution.py:99
  273.7 21.3 %collective-permute-done.1 = bf16[128,8,128]{2,0,1:T(8,128)(2,1)} collective-permute-done((bf16[128,8,128]{2,0,1:T(8,128)(2,1)}, bf16[128,8,128]{2,0,1:T(8,128)(2,1)}, u32[]{:S(2)}, u32[]{:S(2)}) %collective-permute-start.1) | collective-permute-done | bytes 262176 | tf_op jit(solution)/shard_map/while/body/eval_jaxpr/ppermute | solution.py:95
  297.4 13.4 %conditional.2 = (f32[128,8,8,128]{3,0,2,1:T(8,128)}, f32[128,8,128]{2,0,1:T(8,128)S(1)}, f32[128,8,128]{2,0,1:T(8,128)}) conditional(s32[]{:T(128)} %convert_element_type.148, (f32[128,8,8,128]{3,0,2,1:T(8,128)}, bf16[128,8,8,128]{3,0,2,1:T(8,128)(2,1)S(1)}, bf16[128,8,128]{2,0,1:T(8,128)(2,1)S(1)}, f32[128,8,8]{0,2,1:T(8,128)S(1)}, ...), branch_computations={%region_3.3_spmd, %region_4.4_spmd} | conditional | flops 677838848 | bytes 75399248 | solution.py:99
  311.7 21.3 %collective-permute-done.1 = bf16[128,8,128]{2,0,1:T(8,128)(2,1)} collective-permute-done((bf16[128,8,128]{2,0,1:T(8,128)(2,1)}, bf16[128,8,128]{2,0,1:T(8,128)(2,1)}, u32[]{:S(2)}, u32[]{:S(2)}) %collective-permute-start.1) | collective-permute-done | bytes 262176 | tf_op jit(solution)/shard_map/while/body/eval_jaxpr/ppermute | solution.py:95
  335.4 13.4 %conditional.2 = (f32[128,8,8,128]{3,0,2,1:T(8,128)}, f32[128,8,128]{2,0,1:T(8,128)S(1)}, f32[128,8,128]{2,0,1:T(8,128)}) conditional(s32[]{:T(128)} %convert_element_type.148, (f32[128,8,8,128]{3,0,2,1:T(8,128)}, bf16[128,8,8,128]{3,0,2,1:T(8,128)(2,1)S(1)}, bf16[128,8,128]{2,0,1:T(8,128)(2,1)S(1)}, f32[128,8,8]{0,2,1:T(8,128)S(1)}, ...), branch_computations={%region_3.3_spmd, %region_4.4_spmd} | conditional | flops 677838848 | bytes 75399248 | solution.py:99
  349.8 21.3 %collective-permute-done.1 = bf16[128,8,128]{2,0,1:T(8,128)(2,1)} collective-permute-done((bf16[128,8,128]{2,0,1:T(8,128)(2,1)}, bf16[128,8,128]{2,0,1:T(8,128)(2,1)}, u32[]{:S(2)}, u32[]{:S(2)}) %collective-permute-start.1) | collective-permute-done | bytes 262176 | tf_op jit(solution)/shard_map/while/body/eval_jaxpr/ppermute | solution.py:95
  373.5 13.4 %conditional.2 = (f32[128,8,8,128]{3,0,2,1:T(8,128)}, f32[128,8,128]{2,0,1:T(8,128)S(1)}, f32[128,8,128]{2,0,1:T(8,128)}) conditional(s32[]{:T(128)} %convert_element_type.148, (f32[128,8,8,128]{3,0,2,1:T(8,128)}, bf16[128,8,8,128]{3,0,2,1:T(8,128)(2,1)S(1)}, bf16[128,8,128]{2,0,1:T(8,128)(2,1)S(1)}, f32[128,8,8]{0,2,1:T(8,128)S(1)}, ...), branch_computations={%region_3.3_spmd, %region_4.4_spmd} | conditional | flops 677838848 | bytes 75399248 | solution.py:99
  387.8 21.3 %collective-permute-done.1 = bf16[128,8,128]{2,0,1:T(8,128)(2,1)} collective-permute-done((bf16[128,8,128]{2,0,1:T(8,128)(2,1)}, bf16[128,8,128]{2,0,1:T(8,128)(2,1)}, u32[]{:S(2)}, u32[]{:S(2)}) %collective-permute-start.1) | collective-permute-done | bytes 262176 | tf_op jit(solution)/shard_map/while/body/eval_jaxpr/ppermute | solution.py:95
  411.5 13.4 %conditional.2 = (f32[128,8,8,128]{3,0,2,1:T(8,128)}, f32[128,8,128]{2,0,1:T(8,128)S(1)}, f32[128,8,128]{2,0,1:T(8,128)}) conditional(s32[]{:T(128)} %convert_element_type.148, (f32[128,8,8,128]{3,0,2,1:T(8,128)}, bf16[128,8,8,128]{3,0,2,1:T(8,128)(2,1)S(1)}, bf16[128,8,128]{2,0,1:T(8,128)(2,1)S(1)}, f32[128,8,8]{0,2,1:T(8,128)S(1)}, ...), branch_computations={%region_3.3_spmd, %region_4.4_spmd} | conditional | flops 677838848 | bytes 75399248 | solution.py:99
  425.9 21.3 %collective-permute-done.1 = bf16[128,8,128]{2,0,1:T(8,128)(2,1)} collective-permute-done((bf16[128,8,128]{2,0,1:T(8,128)(2,1)}, bf16[128,8,128]{2,0,1:T(8,128)(2,1)}, u32[]{:S(2)}, u32[]{:S(2)}) %collective-permute-start.1) | collective-permute-done | bytes 262176 | tf_op jit(solution)/shard_map/while/body/eval_jaxpr/ppermute | solution.py:95
  449.6 13.4 %conditional.2 = (f32[128,8,8,128]{3,0,2,1:T(8,128)}, f32[128,8,128]{2,0,1:T(8,128)S(1)}, f32[128,8,128]{2,0,1:T(8,128)}) conditional(s32[]{:T(128)} %convert_element_type.148, (f32[128,8,8,128]{3,0,2,1:T(8,128)}, bf16[128,8,8,128]{3,0,2,1:T(8,128)(2,1)S(1)}, bf16[128,8,128]{2,0,1:T(8,128)(2,1)S(1)}, f32[128,8,8]{0,2,1:T(8,128)S(1)}, ...), branch_computations={%region_3.3_spmd, %region_4.4_spmd} | conditional | flops 677838848 | bytes 75399248 | solution.py:99
  463.9 21.3 %collective-permute-done.1 = bf16[128,8,128]{2,0,1:T(8,128)(2,1)} collective-permute-done((bf16[128,8,128]{2,0,1:T(8,128)(2,1)}, bf16[128,8,128]{2,0,1:T(8,128)(2,1)}, u32[]{:S(2)}, u32[]{:S(2)}) %collective-permute-start.1) | collective-permute-done | bytes 262176 | tf_op jit(solution)/shard_map/while/body/eval_jaxpr/ppermute | solution.py:95
  487.6 13.4 %conditional.2 = (f32[128,8,8,128]{3,0,2,1:T(8,128)}, f32[128,8,128]{2,0,1:T(8,128)S(1)}, f32[128,8,128]{2,0,1:T(8,128)}) conditional(s32[]{:T(128)} %convert_element_type.148, (f32[128,8,8,128]{3,0,2,1:T(8,128)}, bf16[128,8,8,128]{3,0,2,1:T(8,128)(2,1)S(1)}, bf16[128,8,128]{2,0,1:T(8,128)(2,1)S(1)}, f32[128,8,8]{0,2,1:T(8,128)S(1)}, ...), branch_computations={%region_3.3_spmd, %region_4.4_spmd} | conditional | flops 677838848 | bytes 75399248 | solution.py:99
  501.9 21.3 %collective-permute-done.1 = bf16[128,8,128]{2,0,1:T(8,128)(2,1)} collective-permute-done((bf16[128,8,128]{2,0,1:T(8,128)(2,1)}, bf16[128,8,128]{2,0,1:T(8,128)(2,1)}, u32[]{:S(2)}, u32[]{:S(2)}) %collective-permute-start.1) | collective-permute-done | bytes 262176 | tf_op jit(solution)/shard_map/while/body/eval_jaxpr/ppermute | solution.py:95
  525.6 13.4 %conditional.2 = (f32[128,8,8,128]{3,0,2,1:T(8,128)}, f32[128,8,128]{2,0,1:T(8,128)S(1)}, f32[128,8,128]{2,0,1:T(8,128)}) conditional(s32[]{:T(128)} %convert_element_type.148, (f32[128,8,8,128]{3,0,2,1:T(8,128)}, bf16[128,8,8,128]{3,0,2,1:T(8,128)(2,1)S(1)}, bf16[128,8,128]{2,0,1:T(8,128)(2,1)S(1)}, f32[128,8,8]{0,2,1:T(8,128)S(1)}, ...), branch_computations={%region_3.3_spmd, %region_4.4_spmd} | conditional | flops 677838848 | bytes 75399248 | solution.py:99
  540.0 21.3 %collective-permute-done.1 = bf16[128,8,128]{2,0,1:T(8,128)(2,1)} collective-permute-done((bf16[128,8,128]{2,0,1:T(8,128)(2,1)}, bf16[128,8,128]{2,0,1:T(8,128)(2,1)}, u32[]{:S(2)}, u32[]{:S(2)}) %collective-permute-start.1) | collective-permute-done | bytes 262176 | tf_op jit(solution)/shard_map/while/body/eval_jaxpr/ppermute | solution.py:95
  563.7 13.4 %conditional.2 = (f32[128,8,8,128]{3,0,2,1:T(8,128)}, f32[128,8,128]{2,0,1:T(8,128)S(1)}, f32[128,8,128]{2,0,1:T(8,128)}) conditional(s32[]{:T(128)} %convert_element_type.148, (f32[128,8,8,128]{3,0,2,1:T(8,128)}, bf16[128,8,8,128]{3,0,2,1:T(8,128)(2,1)S(1)}, bf16[128,8,128]{2,0,1:T(8,128)(2,1)S(1)}, f32[128,8,8]{0,2,1:T(8,128)S(1)}, ...), branch_computations={%region_3.3_spmd, %region_4.4_spmd} | conditional | flops 677838848 | bytes 75399248 | solution.py:99
  578.0 21.3 %collective-permute-done.1 = bf16[128,8,128]{2,0,1:T(8,128)(2,1)} collective-permute-done((bf16[128,8,128]{2,0,1:T(8,128)(2,1)}, bf16[128,8,128]{2,0,1:T(8,128)(2,1)}, u32[]{:S(2)}, u32[]{:S(2)}) %collective-permute-start.1) | collective-permute-done | bytes 262176 | tf_op jit(solution)/shard_map/while/body/eval_jaxpr/ppermute | solution.py:95
  601.7 13.4 %conditional.2 = (f32[128,8,8,128]{3,0,2,1:T(8,128)}, f32[128,8,128]{2,0,1:T(8,128)S(1)}, f32[128,8,128]{2,0,1:T(8,128)}) conditional(s32[]{:T(128)} %convert_element_type.148, (f32[128,8,8,128]{3,0,2,1:T(8,128)}, bf16[128,8,8,128]{3,0,2,1:T(8,128)(2,1)S(1)}, bf16[128,8,128]{2,0,1:T(8,128)(2,1)S(1)}, f32[128,8,8]{0,2,1:T(8,128)S(1)}, ...), branch_computations={%region_3.3_spmd, %region_4.4_spmd} | conditional | flops 677838848 | bytes 75399248 | solution.py:99
  616.0 21.3 %collective-permute-done.1 = bf16[128,8,128]{2,0,1:T(8,128)(2,1)} collective-permute-done((bf16[128,8,128]{2,0,1:T(8,128)(2,1)}, bf16[128,8,128]{2,0,1:T(8,128)(2,1)}, u32[]{:S(2)}, u32[]{:S(2)}) %collective-permute-start.1) | collective-permute-done | bytes 262176 | tf_op jit(solution)/shard_map/while/body/eval_jaxpr/ppermute | solution.py:95
  639.7 13.4 %conditional.2 = (f32[128,8,8,128]{3,0,2,1:T(8,128)}, f32[128,8,128]{2,0,1:T(8,128)S(1)}, f32[128,8,128]{2,0,1:T(8,128)}) conditional(s32[]{:T(128)} %convert_element_type.148, (f32[128,8,8,128]{3,0,2,1:T(8,128)}, bf16[128,8,8,128]{3,0,2,1:T(8,128)(2,1)S(1)}, bf16[128,8,128]{2,0,1:T(8,128)(2,1)S(1)}, f32[128,8,8]{0,2,1:T(8,128)S(1)}, ...), branch_computations={%region_3.3_spmd, %region_4.4_spmd} | conditional | flops 677838848 | bytes 75399248 | solution.py:99
  654.1 21.3 %collective-permute-done.1 = bf16[128,8,128]{2,0,1:T(8,128)(2,1)} collective-permute-done((bf16[128,8,128]{2,0,1:T(8,128)(2,1)}, bf16[128,8,128]{2,0,1:T(8,128)(2,1)}, u32[]{:S(2)}, u32[]{:S(2)}) %collective-permute-start.1) | collective-permute-done | bytes 262176 | tf_op jit(solution)/shard_map/while/body/eval_jaxpr/ppermute | solution.py:95
  677.8 13.4 %conditional.2 = (f32[128,8,8,128]{3,0,2,1:T(8,128)}, f32[128,8,128]{2,0,1:T(8,128)S(1)}, f32[128,8,128]{2,0,1:T(8,128)}) conditional(s32[]{:T(128)} %convert_element_type.148, (f32[128,8,8,128]{3,0,2,1:T(8,128)}, bf16[128,8,8,128]{3,0,2,1:T(8,128)(2,1)S(1)}, bf16[128,8,128]{2,0,1:T(8,128)(2,1)S(1)}, f32[128,8,8]{0,2,1:T(8,128)S(1)}, ...), branch_computations={%region_3.3_spmd, %region_4.4_spmd} | conditional | flops 677838848 | bytes 75399248 | solution.py:99
  692.1 21.3 %collective-permute-done.1 = bf16[128,8,128]{2,0,1:T(8,128)(2,1)} collective-permute-done((bf16[128,8,128]{2,0,1:T(8,128)(2,1)}, bf16[128,8,128]{2,0,1:T(8,128)(2,1)}, u32[]{:S(2)}, u32[]{:S(2)}) %collective-permute-start.1) | collective-permute-done | bytes 262176 | tf_op jit(solution)/shard_map/while/body/eval_jaxpr/ppermute | solution.py:95
  715.8 13.4 %conditional.2 = (f32[128,8,8,128]{3,0,2,1:T(8,128)}, f32[128,8,128]{2,0,1:T(8,128)S(1)}, f32[128,8,128]{2,0,1:T(8,128)}) conditional(s32[]{:T(128)} %convert_element_type.148, (f32[128,8,8,128]{3,0,2,1:T(8,128)}, bf16[128,8,8,128]{3,0,2,1:T(8,128)(2,1)S(1)}, bf16[128,8,128]{2,0,1:T(8,128)(2,1)S(1)}, f32[128,8,8]{0,2,1:T(8,128)S(1)}, ...), branch_computations={%region_3.3_spmd, %region_4.4_spmd} | conditional | flops 677838848 | bytes 75399248 | solution.py:99
  730.2 21.3 %collective-permute-done.1 = bf16[128,8,128]{2,0,1:T(8,128)(2,1)} collective-permute-done((bf16[128,8,128]{2,0,1:T(8,128)(2,1)}, bf16[128,8,128]{2,0,1:T(8,128)(2,1)}, u32[]{:S(2)}, u32[]{:S(2)}) %collective-permute-start.1) | collective-permute-done | bytes 262176 | tf_op jit(solution)/shard_map/while/body/eval_jaxpr/ppermute | solution.py:95
  753.9 13.4 %conditional.2 = (f32[128,8,8,128]{3,0,2,1:T(8,128)}, f32[128,8,128]{2,0,1:T(8,128)S(1)}, f32[128,8,128]{2,0,1:T(8,128)}) conditional(s32[]{:T(128)} %convert_element_type.148, (f32[128,8,8,128]{3,0,2,1:T(8,128)}, bf16[128,8,8,128]{3,0,2,1:T(8,128)(2,1)S(1)}, bf16[128,8,128]{2,0,1:T(8,128)(2,1)S(1)}, f32[128,8,8]{0,2,1:T(8,128)S(1)}, ...), branch_computations={%region_3.3_spmd, %region_4.4_spmd} | conditional | flops 677838848 | bytes 75399248 | solution.py:99
  768.2 21.3 %collective-permute-done.1 = bf16[128,8,128]{2,0,1:T(8,128)(2,1)} collective-permute-done((bf16[128,8,128]{2,0,1:T(8,128)(2,1)}, bf16[128,8,128]{2,0,1:T(8,128)(2,1)}, u32[]{:S(2)}, u32[]{:S(2)}) %collective-permute-start.1) | collective-permute-done | bytes 262176 | tf_op jit(solution)/shard_map/while/body/eval_jaxpr/ppermute | solution.py:95
  791.9 13.4 %conditional.2 = (f32[128,8,8,128]{3,0,2,1:T(8,128)}, f32[128,8,128]{2,0,1:T(8,128)S(1)}, f32[128,8,128]{2,0,1:T(8,128)}) conditional(s32[]{:T(128)} %convert_element_type.148, (f32[128,8,8,128]{3,0,2,1:T(8,128)}, bf16[128,8,8,128]{3,0,2,1:T(8,128)(2,1)S(1)}, bf16[128,8,128]{2,0,1:T(8,128)(2,1)S(1)}, f32[128,8,8]{0,2,1:T(8,128)S(1)}, ...), branch_computations={%region_3.3_spmd, %region_4.4_spmd} | conditional | flops 677838848 | bytes 75399248 | solution.py:99
  806.2 21.3 %collective-permute-done.1 = bf16[128,8,128]{2,0,1:T(8,128)(2,1)} collective-permute-done((bf16[128,8,128]{2,0,1:T(8,128)(2,1)}, bf16[128,8,128]{2,0,1:T(8,128)(2,1)}, u32[]{:S(2)}, u32[]{:S(2)}) %collective-permute-start.1) | collective-permute-done | bytes 262176 | tf_op jit(solution)/shard_map/while/body/eval_jaxpr/ppermute | solution.py:95
  829.9 13.4 %conditional.2 = (f32[128,8,8,128]{3,0,2,1:T(8,128)}, f32[128,8,128]{2,0,1:T(8,128)S(1)}, f32[128,8,128]{2,0,1:T(8,128)}) conditional(s32[]{:T(128)} %convert_element_type.148, (f32[128,8,8,128]{3,0,2,1:T(8,128)}, bf16[128,8,8,128]{3,0,2,1:T(8,128)(2,1)S(1)}, bf16[128,8,128]{2,0,1:T(8,128)(2,1)S(1)}, f32[128,8,8]{0,2,1:T(8,128)S(1)}, ...), branch_computations={%region_3.3_spmd, %region_4.4_spmd} | conditional | flops 677838848 | bytes 75399248 | solution.py:99
  844.3 21.3 %collective-permute-done.1 = bf16[128,8,128]{2,0,1:T(8,128)(2,1)} collective-permute-done((bf16[128,8,128]{2,0,1:T(8,128)(2,1)}, bf16[128,8,128]{2,0,1:T(8,128)(2,1)}, u32[]{:S(2)}, u32[]{:S(2)}) %collective-permute-start.1) | collective-permute-done | bytes 262176 | tf_op jit(solution)/shard_map/while/body/eval_jaxpr/ppermute | solution.py:95
  868.0 13.4 %conditional.2 = (f32[128,8,8,128]{3,0,2,1:T(8,128)}, f32[128,8,128]{2,0,1:T(8,128)S(1)}, f32[128,8,128]{2,0,1:T(8,128)}) conditional(s32[]{:T(128)} %convert_element_type.148, (f32[128,8,8,128]{3,0,2,1:T(8,128)}, bf16[128,8,8,128]{3,0,2,1:T(8,128)(2,1)S(1)}, bf16[128,8,128]{2,0,1:T(8,128)(2,1)S(1)}, f32[128,8,8]{0,2,1:T(8,128)S(1)}, ...), branch_computations={%region_3.3_spmd, %region_4.4_spmd} | conditional | flops 677838848 | bytes 75399248 | solution.py:99
  882.3 21.3 %collective-permute-done.1 = bf16[128,8,128]{2,0,1:T(8,128)(2,1)} collective-permute-done((bf16[128,8,128]{2,0,1:T(8,128)(2,1)}, bf16[128,8,128]{2,0,1:T(8,128)(2,1)}, u32[]{:S(2)}, u32[]{:S(2)}) %collective-permute-start.1) | collective-permute-done | bytes 262176 | tf_op jit(solution)/shard_map/while/body/eval_jaxpr/ppermute | solution.py:95
  906.0 13.4 %conditional.2 = (f32[128,8,8,128]{3,0,2,1:T(8,128)}, f32[128,8,128]{2,0,1:T(8,128)S(1)}, f32[128,8,128]{2,0,1:T(8,128)}) conditional(s32[]{:T(128)} %convert_element_type.148, (f32[128,8,8,128]{3,0,2,1:T(8,128)}, bf16[128,8,8,128]{3,0,2,1:T(8,128)(2,1)S(1)}, bf16[128,8,128]{2,0,1:T(8,128)(2,1)S(1)}, f32[128,8,8]{0,2,1:T(8,128)S(1)}, ...), branch_computations={%region_3.3_spmd, %region_4.4_spmd} | conditional | flops 677838848 | bytes 75399248 | solution.py:99
  920.3 21.3 %collective-permute-done.1 = bf16[128,8,128]{2,0,1:T(8,128)(2,1)} collective-permute-done((bf16[128,8,128]{2,0,1:T(8,128)(2,1)}, bf16[128,8,128]{2,0,1:T(8,128)(2,1)}, u32[]{:S(2)}, u32[]{:S(2)}) %collective-permute-start.1) | collective-permute-done | bytes 262176 | tf_op jit(solution)/shard_map/while/body/eval_jaxpr/ppermute | solution.py:95
  944.0 13.4 %conditional.2 = (f32[128,8,8,128]{3,0,2,1:T(8,128)}, f32[128,8,128]{2,0,1:T(8,128)S(1)}, f32[128,8,128]{2,0,1:T(8,128)}) conditional(s32[]{:T(128)} %convert_element_type.148, (f32[128,8,8,128]{3,0,2,1:T(8,128)}, bf16[128,8,8,128]{3,0,2,1:T(8,128)(2,1)S(1)}, bf16[128,8,128]{2,0,1:T(8,128)(2,1)S(1)}, f32[128,8,8]{0,2,1:T(8,128)S(1)}, ...), branch_computations={%region_3.3_spmd, %region_4.4_spmd} | conditional | flops 677838848 | bytes 75399248 | solution.py:99
  958.4 21.3 %collective-permute-done.1 = bf16[128,8,128]{2,0,1:T(8,128)(2,1)} collective-permute-done((bf16[128,8,128]{2,0,1:T(8,128)(2,1)}, bf16[128,8,128]{2,0,1:T(8,128)(2,1)}, u32[]{:S(2)}, u32[]{:S(2)}) %collective-permute-start.1) | collective-permute-done | bytes 262176 | tf_op jit(solution)/shard_map/while/body/eval_jaxpr/ppermute | solution.py:95
  982.1 13.4 %conditional.2 = (f32[128,8,8,128]{3,0,2,1:T(8,128)}, f32[128,8,128]{2,0,1:T(8,128)S(1)}, f32[128,8,128]{2,0,1:T(8,128)}) conditional(s32[]{:T(128)} %convert_element_type.148, (f32[128,8,8,128]{3,0,2,1:T(8,128)}, bf16[128,8,8,128]{3,0,2,1:T(8,128)(2,1)S(1)}, bf16[128,8,128]{2,0,1:T(8,128)(2,1)S(1)}, f32[128,8,8]{0,2,1:T(8,128)S(1)}, ...), branch_computations={%region_3.3_spmd, %region_4.4_spmd} | conditional | flops 677838848 | bytes 75399248 | solution.py:99
  996.4 21.3 %collective-permute-done.1 = bf16[128,8,128]{2,0,1:T(8,128)(2,1)} collective-permute-done((bf16[128,8,128]{2,0,1:T(8,128)(2,1)}, bf16[128,8,128]{2,0,1:T(8,128)(2,1)}, u32[]{:S(2)}, u32[]{:S(2)}) %collective-permute-start.1) | collective-permute-done | bytes 262176 | tf_op jit(solution)/shard_map/while/body/eval_jaxpr/ppermute | solution.py:95
  1020.1 13.4 %conditional.2 = (f32[128,8,8,128]{3,0,2,1:T(8,128)}, f32[128,8,128]{2,0,1:T(8,128)S(1)}, f32[128,8,128]{2,0,1:T(8,128)}) conditional(s32[]{:T(128)} %convert_element_type.148, (f32[128,8,8,128]{3,0,2,1:T(8,128)}, bf16[128,8,8,128]{3,0,2,1:T(8,128)(2,1)S(1)}, bf16[128,8,128]{2,0,1:T(8,128)(2,1)S(1)}, f32[128,8,8]{0,2,1:T(8,128)S(1)}, ...), branch_computations={%region_3.3_spmd, %region_4.4_spmd} | conditional | flops 677838848 | bytes 75399248 | solution.py:99
  1034.5 21.3 %collective-permute-done.1 = bf16[128,8,128]{2,0,1:T(8,128)(2,1)} collective-permute-done((bf16[128,8,128]{2,0,1:T(8,128)(2,1)}, bf16[128,8,128]{2,0,1:T(8,128)(2,1)}, u32[]{:S(2)}, u32[]{:S(2)}) %collective-permute-start.1) | collective-permute-done | bytes 262176 | tf_op jit(solution)/shard_map/while/body/eval_jaxpr/ppermute | solution.py:95
  1058.2 13.4 %conditional.2 = (f32[128,8,8,128]{3,0,2,1:T(8,128)}, f32[128,8,128]{2,0,1:T(8,128)S(1)}, f32[128,8,128]{2,0,1:T(8,128)}) conditional(s32[]{:T(128)} %convert_element_type.148, (f32[128,8,8,128]{3,0,2,1:T(8,128)}, bf16[128,8,8,128]{3,0,2,1:T(8,128)(2,1)S(1)}, bf16[128,8,128]{2,0,1:T(8,128)(2,1)S(1)}, f32[128,8,8]{0,2,1:T(8,128)S(1)}, ...), branch_computations={%region_3.3_spmd, %region_4.4_spmd} | conditional | flops 677838848 | bytes 75399248 | solution.py:99
  1072.5 21.3 %collective-permute-done.1 = bf16[128,8,128]{2,0,1:T(8,128)(2,1)} collective-permute-done((bf16[128,8,128]{2,0,1:T(8,128)(2,1)}, bf16[128,8,128]{2,0,1:T(8,128)(2,1)}, u32[]{:S(2)}, u32[]{:S(2)}) %collective-permute-start.1) | collective-permute-done | bytes 262176 | tf_op jit(solution)/shard_map/while/body/eval_jaxpr/ppermute | solution.py:95
  1096.2 13.4 %conditional.2 = (f32[128,8,8,128]{3,0,2,1:T(8,128)}, f32[128,8,128]{2,0,1:T(8,128)S(1)}, f32[128,8,128]{2,0,1:T(8,128)}) conditional(s32[]{:T(128)} %convert_element_type.148, (f32[128,8,8,128]{3,0,2,1:T(8,128)}, bf16[128,8,8,128]{3,0,2,1:T(8,128)(2,1)S(1)}, bf16[128,8,128]{2,0,1:T(8,128)(2,1)S(1)}, f32[128,8,8]{0,2,1:T(8,128)S(1)}, ...), branch_computations={%region_3.3_spmd, %region_4.4_spmd} | conditional | flops 677838848 | bytes 75399248 | solution.py:99
  1110.5 21.3 %collective-permute-done.1 = bf16[128,8,128]{2,0,1:T(8,128)(2,1)} collective-permute-done((bf16[128,8,128]{2,0,1:T(8,128)(2,1)}, bf16[128,8,128]{2,0,1:T(8,128)(2,1)}, u32[]{:S(2)}, u32[]{:S(2)}) %collective-permute-start.1) | collective-permute-done | bytes 262176 | tf_op jit(solution)/shard_map/while/body/eval_jaxpr/ppermute | solution.py:95
  1134.2 13.4 %conditional.2 = (f32[128,8,8,128]{3,0,2,1:T(8,128)}, f32[128,8,128]{2,0,1:T(8,128)S(1)}, f32[128,8,128]{2,0,1:T(8,128)}) conditional(s32[]{:T(128)} %convert_element_type.148, (f32[128,8,8,128]{3,0,2,1:T(8,128)}, bf16[128,8,8,128]{3,0,2,1:T(8,128)(2,1)S(1)}, bf16[128,8,128]{2,0,1:T(8,128)(2,1)S(1)}, f32[128,8,8]{0,2,1:T(8,128)S(1)}, ...), branch_computations={%region_3.3_spmd, %region_4.4_spmd} | conditional | flops 677838848 | bytes 75399248 | solution.py:99
  1148.6 21.3 %collective-permute-done.1 = bf16[128,8,128]{2,0,1:T(8,128)(2,1)} collective-permute-done((bf16[128,8,128]{2,0,1:T(8,128)(2,1)}, bf16[128,8,128]{2,0,1:T(8,128)(2,1)}, u32[]{:S(2)}, u32[]{:S(2)}) %collective-permute-start.1) | collective-permute-done | bytes 262176 | tf_op jit(solution)/shard_map/while/body/eval_jaxpr/ppermute | solution.py:95
  1172.3 13.4 %conditional.2 = (f32[128,8,8,128]{3,0,2,1:T(8,128)}, f32[128,8,128]{2,0,1:T(8,128)S(1)}, f32[128,8,128]{2,0,1:T(8,128)}) conditional(s32[]{:T(128)} %convert_element_type.148, (f32[128,8,8,128]{3,0,2,1:T(8,128)}, bf16[128,8,8,128]{3,0,2,1:T(8,128)(2,1)S(1)}, bf16[128,8,128]{2,0,1:T(8,128)(2,1)S(1)}, f32[128,8,8]{0,2,1:T(8,128)S(1)}, ...), branch_computations={%region_3.3_spmd, %region_4.4_spmd} | conditional | flops 677838848 | bytes 75399248 | solution.py:99
  1186.6 21.3 %collective-permute-done.1 = bf16[128,8,128]{2,0,1:T(8,128)(2,1)} collective-permute-done((bf16[128,8,128]{2,0,1:T(8,128)(2,1)}, bf16[128,8,128]{2,0,1:T(8,128)(2,1)}, u32[]{:S(2)}, u32[]{:S(2)}) %collective-permute-start.1) | collective-permute-done | bytes 262176 | tf_op jit(solution)/shard_map/while/body/eval_jaxpr/ppermute | solution.py:95
  1210.3 13.4 %conditional.2 = (f32[128,8,8,128]{3,0,2,1:T(8,128)}, f32[128,8,128]{2,0,1:T(8,128)S(1)}, f32[128,8,128]{2,0,1:T(8,128)}) conditional(s32[]{:T(128)} %convert_element_type.148, (f32[128,8,8,128]{3,0,2,1:T(8,128)}, bf16[128,8,8,128]{3,0,2,1:T(8,128)(2,1)S(1)}, bf16[128,8,128]{2,0,1:T(8,128)(2,1)S(1)}, f32[128,8,8]{0,2,1:T(8,128)S(1)}, ...), branch_computations={%region_3.3_spmd, %region_4.4_spmd} | conditional | flops 677838848 | bytes 75399248 | solution.py:99
  1249.0 65.6 %all-reduce.4 = (f32[128]{0:T(128)}, f32[128]{0:T(128)}) all-reduce(f32[128]{0:T(128)S(1)} %get-tuple-element.421, f32[128]{0:T(128)S(1)} %get-tuple-element.423), channel_id=1, replica_groups=mesh['dp'=1,'cp'=32] {'cp'}, use_global_device_ids=true, to_apply=%region_9.10 | all-reduce | flops 256 | bytes 2048 | tf_op jit(solution)/shard_map/psum | solution.py:109
  (930 shorter events, 612.0 us)
Async XLA Ops:
  159.9 23.4 %collective-permute-start.3 = (f32[128,8,128]{2,0,1:T(8,128)}, f32[128,8,128]{2,0,1:T(8,128)S(1)}, u32[]{:S(2)}, u32[]{:S(2)}) collective-permute-start(f32[128,8,128]{2,0,1:T(8,128)} %get-tuple-element.592), channel_id=1, source_target_pairs={{0,1},{1,2},{2,3},{3,4},{4,5},{5,6},{6,7},{7,8},{8,9},{9,10},{10,1... | collective-permute-start | bytes 1572872 | tf_op jit(solution)/shard_map/while/body/eval_jaxpr/ppermute | solution.py:97
  197.5 23.9 %collective-permute-start.3 = (f32[128,8,128]{2,0,1:T(8,128)}, f32[128,8,128]{2,0,1:T(8,128)S(1)}, u32[]{:S(2)}, u32[]{:S(2)}) collective-permute-start(f32[128,8,128]{2,0,1:T(8,128)} %get-tuple-element.592), channel_id=1, source_target_pairs={{0,1},{1,2},{2,3},{3,4},{4,5},{5,6},{6,7},{7,8},{8,9},{9,10},{10,1... | collective-permute-start | bytes 1572872 | tf_op jit(solution)/shard_map/while/body/eval_jaxpr/ppermute | solution.py:97
  197.5 23.9 %collective-permute-start.2 = (f32[128,8,128]{2,0,1:T(8,128)}, f32[128,8,128]{2,0,1:T(8,128)S(1)}, u32[]{:S(2)}, u32[]{:S(2)}) collective-permute-start(f32[128,8,128]{2,0,1:T(8,128)} %get-tuple-element.591), channel_id=1, source_target_pairs={{0,1},{1,2},{2,3},{3,4},{4,5},{5,6},{6,7},{7,8},{8,9},{9,10},{10,1... | collective-permute-start | bytes 1572872 | tf_op jit(solution)/shard_map/while/body/eval_jaxpr/ppermute | solution.py:96
  197.5 23.1 %collective-permute-start = (bf16[128,8,128]{2,0,1:T(8,128)(2,1)}, bf16[128,8,128]{2,0,1:T(8,128)(2,1)S(1)}, u32[]{:S(2)}, u32[]{:S(2)}) collective-permute-start(bf16[128,8,128]{2,0,1:T(8,128)(2,1)} %get-tuple-element.588), channel_id=1, source_target_pairs={{0,1},{1,2},{2,3},{3,4},{4,5},{5,6},{6,7},{7,8},{8,9},{9,10},{10,1... | collective-permute-start | bytes 786440 | tf_op jit(solution)/shard_map/while/body/eval_jaxpr/ppermute | solution.py:94
  235.5 23.9 %collective-permute-start.3 = (f32[128,8,128]{2,0,1:T(8,128)}, f32[128,8,128]{2,0,1:T(8,128)S(1)}, u32[]{:S(2)}, u32[]{:S(2)}) collective-permute-start(f32[128,8,128]{2,0,1:T(8,128)} %get-tuple-element.592), channel_id=1, source_target_pairs={{0,1},{1,2},{2,3},{3,4},{4,5},{5,6},{6,7},{7,8},{8,9},{9,10},{10,1... | collective-permute-start | bytes 1572872 | tf_op jit(solution)/shard_map/while/body/eval_jaxpr/ppermute | solution.py:97
  235.5 23.9 %collective-permute-start.2 = (f32[128,8,128]{2,0,1:T(8,128)}, f32[128,8,128]{2,0,1:T(8,128)S(1)}, u32[]{:S(2)}, u32[]{:S(2)}) collective-permute-start(f32[128,8,128]{2,0,1:T(8,128)} %get-tuple-element.591), channel_id=1, source_target_pairs={{0,1},{1,2},{2,3},{3,4},{4,5},{5,6},{6,7},{7,8},{8,9},{9,10},{10,1... | collective-permute-start | bytes 1572872 | tf_op jit(solution)/shard_map/while/body/eval_jaxpr/ppermute | solution.py:96
  235.5 23.1 %collective-permute-start = (bf16[128,8,128]{2,0,1:T(8,128)(2,1)}, bf16[128,8,128]{2,0,1:T(8,128)(2,1)S(1)}, u32[]{:S(2)}, u32[]{:S(2)}) collective-permute-start(bf16[128,8,128]{2,0,1:T(8,128)(2,1)} %get-tuple-element.588), channel_id=1, source_target_pairs={{0,1},{1,2},{2,3},{3,4},{4,5},{5,6},{6,7},{7,8},{8,9},{9,10},{10,1... | collective-permute-start | bytes 786440 | tf_op jit(solution)/shard_map/while/body/eval_jaxpr/ppermute | solution.py:94
  273.5 23.9 %collective-permute-start.3 = (f32[128,8,128]{2,0,1:T(8,128)}, f32[128,8,128]{2,0,1:T(8,128)S(1)}, u32[]{:S(2)}, u32[]{:S(2)}) collective-permute-start(f32[128,8,128]{2,0,1:T(8,128)} %get-tuple-element.592), channel_id=1, source_target_pairs={{0,1},{1,2},{2,3},{3,4},{4,5},{5,6},{6,7},{7,8},{8,9},{9,10},{10,1... | collective-permute-start | bytes 1572872 | tf_op jit(solution)/shard_map/while/body/eval_jaxpr/ppermute | solution.py:97
  273.5 23.9 %collective-permute-start.2 = (f32[128,8,128]{2,0,1:T(8,128)}, f32[128,8,128]{2,0,1:T(8,128)S(1)}, u32[]{:S(2)}, u32[]{:S(2)}) collective-permute-start(f32[128,8,128]{2,0,1:T(8,128)} %get-tuple-element.591), channel_id=1, source_target_pairs={{0,1},{1,2},{2,3},{3,4},{4,5},{5,6},{6,7},{7,8},{8,9},{9,10},{10,1... | collective-permute-start | bytes 1572872 | tf_op jit(solution)/shard_map/while/body/eval_jaxpr/ppermute | solution.py:96
  273.6 23.1 %collective-permute-start = (bf16[128,8,128]{2,0,1:T(8,128)(2,1)}, bf16[128,8,128]{2,0,1:T(8,128)(2,1)S(1)}, u32[]{:S(2)}, u32[]{:S(2)}) collective-permute-start(bf16[128,8,128]{2,0,1:T(8,128)(2,1)} %get-tuple-element.588), channel_id=1, source_target_pairs={{0,1},{1,2},{2,3},{3,4},{4,5},{5,6},{6,7},{7,8},{8,9},{9,10},{10,1... | collective-permute-start | bytes 786440 | tf_op jit(solution)/shard_map/while/body/eval_jaxpr/ppermute | solution.py:94
  311.6 23.9 %collective-permute-start.3 = (f32[128,8,128]{2,0,1:T(8,128)}, f32[128,8,128]{2,0,1:T(8,128)S(1)}, u32[]{:S(2)}, u32[]{:S(2)}) collective-permute-start(f32[128,8,128]{2,0,1:T(8,128)} %get-tuple-element.592), channel_id=1, source_target_pairs={{0,1},{1,2},{2,3},{3,4},{4,5},{5,6},{6,7},{7,8},{8,9},{9,10},{10,1... | collective-permute-start | bytes 1572872 | tf_op jit(solution)/shard_map/while/body/eval_jaxpr/ppermute | solution.py:97
  311.6 23.9 %collective-permute-start.2 = (f32[128,8,128]{2,0,1:T(8,128)}, f32[128,8,128]{2,0,1:T(8,128)S(1)}, u32[]{:S(2)}, u32[]{:S(2)}) collective-permute-start(f32[128,8,128]{2,0,1:T(8,128)} %get-tuple-element.591), channel_id=1, source_target_pairs={{0,1},{1,2},{2,3},{3,4},{4,5},{5,6},{6,7},{7,8},{8,9},{9,10},{10,1... | collective-permute-start | bytes 1572872 | tf_op jit(solution)/shard_map/while/body/eval_jaxpr/ppermute | solution.py:96
  311.6 23.1 %collective-permute-start = (bf16[128,8,128]{2,0,1:T(8,128)(2,1)}, bf16[128,8,128]{2,0,1:T(8,128)(2,1)S(1)}, u32[]{:S(2)}, u32[]{:S(2)}) collective-permute-start(bf16[128,8,128]{2,0,1:T(8,128)(2,1)} %get-tuple-element.588), channel_id=1, source_target_pairs={{0,1},{1,2},{2,3},{3,4},{4,5},{5,6},{6,7},{7,8},{8,9},{9,10},{10,1... | collective-permute-start | bytes 786440 | tf_op jit(solution)/shard_map/while/body/eval_jaxpr/ppermute | solution.py:94
  349.6 23.9 %collective-permute-start.3 = (f32[128,8,128]{2,0,1:T(8,128)}, f32[128,8,128]{2,0,1:T(8,128)S(1)}, u32[]{:S(2)}, u32[]{:S(2)}) collective-permute-start(f32[128,8,128]{2,0,1:T(8,128)} %get-tuple-element.592), channel_id=1, source_target_pairs={{0,1},{1,2},{2,3},{3,4},{4,5},{5,6},{6,7},{7,8},{8,9},{9,10},{10,1... | collective-permute-start | bytes 1572872 | tf_op jit(solution)/shard_map/while/body/eval_jaxpr/ppermute | solution.py:97
  349.6 23.9 %collective-permute-start.2 = (f32[128,8,128]{2,0,1:T(8,128)}, f32[128,8,128]{2,0,1:T(8,128)S(1)}, u32[]{:S(2)}, u32[]{:S(2)}) collective-permute-start(f32[128,8,128]{2,0,1:T(8,128)} %get-tuple-element.591), channel_id=1, source_target_pairs={{0,1},{1,2},{2,3},{3,4},{4,5},{5,6},{6,7},{7,8},{8,9},{9,10},{10,1... | collective-permute-start | bytes 1572872 | tf_op jit(solution)/shard_map/while/body/eval_jaxpr/ppermute | solution.py:96
  349.6 23.1 %collective-permute-start = (bf16[128,8,128]{2,0,1:T(8,128)(2,1)}, bf16[128,8,128]{2,0,1:T(8,128)(2,1)S(1)}, u32[]{:S(2)}, u32[]{:S(2)}) collective-permute-start(bf16[128,8,128]{2,0,1:T(8,128)(2,1)} %get-tuple-element.588), channel_id=1, source_target_pairs={{0,1},{1,2},{2,3},{3,4},{4,5},{5,6},{6,7},{7,8},{8,9},{9,10},{10,1... | collective-permute-start | bytes 786440 | tf_op jit(solution)/shard_map/while/body/eval_jaxpr/ppermute | solution.py:94
  387.7 23.9 %collective-permute-start.3 = (f32[128,8,128]{2,0,1:T(8,128)}, f32[128,8,128]{2,0,1:T(8,128)S(1)}, u32[]{:S(2)}, u32[]{:S(2)}) collective-permute-start(f32[128,8,128]{2,0,1:T(8,128)} %get-tuple-element.592), channel_id=1, source_target_pairs={{0,1},{1,2},{2,3},{3,4},{4,5},{5,6},{6,7},{7,8},{8,9},{9,10},{10,1... | collective-permute-start | bytes 1572872 | tf_op jit(solution)/shard_map/while/body/eval_jaxpr/ppermute | solution.py:97
  387.7 23.9 %collective-permute-start.2 = (f32[128,8,128]{2,0,1:T(8,128)}, f32[128,8,128]{2,0,1:T(8,128)S(1)}, u32[]{:S(2)}, u32[]{:S(2)}) collective-permute-start(f32[128,8,128]{2,0,1:T(8,128)} %get-tuple-element.591), channel_id=1, source_target_pairs={{0,1},{1,2},{2,3},{3,4},{4,5},{5,6},{6,7},{7,8},{8,9},{9,10},{10,1... | collective-permute-start | bytes 1572872 | tf_op jit(solution)/shard_map/while/body/eval_jaxpr/ppermute | solution.py:96
  387.7 23.1 %collective-permute-start = (bf16[128,8,128]{2,0,1:T(8,128)(2,1)}, bf16[128,8,128]{2,0,1:T(8,128)(2,1)S(1)}, u32[]{:S(2)}, u32[]{:S(2)}) collective-permute-start(bf16[128,8,128]{2,0,1:T(8,128)(2,1)} %get-tuple-element.588), channel_id=1, source_target_pairs={{0,1},{1,2},{2,3},{3,4},{4,5},{5,6},{6,7},{7,8},{8,9},{9,10},{10,1... | collective-permute-start | bytes 786440 | tf_op jit(solution)/shard_map/while/body/eval_jaxpr/ppermute | solution.py:94
  425.7 23.9 %collective-permute-start.3 = (f32[128,8,128]{2,0,1:T(8,128)}, f32[128,8,128]{2,0,1:T(8,128)S(1)}, u32[]{:S(2)}, u32[]{:S(2)}) collective-permute-start(f32[128,8,128]{2,0,1:T(8,128)} %get-tuple-element.592), channel_id=1, source_target_pairs={{0,1},{1,2},{2,3},{3,4},{4,5},{5,6},{6,7},{7,8},{8,9},{9,10},{10,1... | collective-permute-start | bytes 1572872 | tf_op jit(solution)/shard_map/while/body/eval_jaxpr/ppermute | solution.py:97
  425.7 23.9 %collective-permute-start.2 = (f32[128,8,128]{2,0,1:T(8,128)}, f32[128,8,128]{2,0,1:T(8,128)S(1)}, u32[]{:S(2)}, u32[]{:S(2)}) collective-permute-start(f32[128,8,128]{2,0,1:T(8,128)} %get-tuple-element.591), channel_id=1, source_target_pairs={{0,1},{1,2},{2,3},{3,4},{4,5},{5,6},{6,7},{7,8},{8,9},{9,10},{10,1... | collective-permute-start | bytes 1572872 | tf_op jit(solution)/shard_map/while/body/eval_jaxpr/ppermute | solution.py:96
  425.7 23.1 %collective-permute-start = (bf16[128,8,128]{2,0,1:T(8,128)(2,1)}, bf16[128,8,128]{2,0,1:T(8,128)(2,1)S(1)}, u32[]{:S(2)}, u32[]{:S(2)}) collective-permute-start(bf16[128,8,128]{2,0,1:T(8,128)(2,1)} %get-tuple-element.588), channel_id=1, source_target_pairs={{0,1},{1,2},{2,3},{3,4},{4,5},{5,6},{6,7},{7,8},{8,9},{9,10},{10,1... | collective-permute-start | bytes 786440 | tf_op jit(solution)/shard_map/while/body/eval_jaxpr/ppermute | solution.py:94
  463.7 23.9 %collective-permute-start.3 = (f32[128,8,128]{2,0,1:T(8,128)}, f32[128,8,128]{2,0,1:T(8,128)S(1)}, u32[]{:S(2)}, u32[]{:S(2)}) collective-permute-start(f32[128,8,128]{2,0,1:T(8,128)} %get-tuple-element.592), channel_id=1, source_target_pairs={{0,1},{1,2},{2,3},{3,4},{4,5},{5,6},{6,7},{7,8},{8,9},{9,10},{10,1... | collective-permute-start | bytes 1572872 | tf_op jit(solution)/shard_map/while/body/eval_jaxpr/ppermute | solution.py:97
  463.7 23.9 %collective-permute-start.2 = (f32[128,8,128]{2,0,1:T(8,128)}, f32[128,8,128]{2,0,1:T(8,128)S(1)}, u32[]{:S(2)}, u32[]{:S(2)}) collective-permute-start(f32[128,8,128]{2,0,1:T(8,128)} %get-tuple-element.591), channel_id=1, source_target_pairs={{0,1},{1,2},{2,3},{3,4},{4,5},{5,6},{6,7},{7,8},{8,9},{9,10},{10,1... | collective-permute-start | bytes 1572872 | tf_op jit(solution)/shard_map/while/body/eval_jaxpr/ppermute | solution.py:96
  501.8 23.9 %collective-permute-start.3 = (f32[128,8,128]{2,0,1:T(8,128)}, f32[128,8,128]{2,0,1:T(8,128)S(1)}, u32[]{:S(2)}, u32[]{:S(2)}) collective-permute-start(f32[128,8,128]{2,0,1:T(8,128)} %get-tuple-element.592), channel_id=1, source_target_pairs={{0,1},{1,2},{2,3},{3,4},{4,5},{5,6},{6,7},{7,8},{8,9},{9,10},{10,1... | collective-permute-start | bytes 1572872 | tf_op jit(solution)/shard_map/while/body/eval_jaxpr/ppermute | solution.py:97
  501.8 23.9 %collective-permute-start.2 = (f32[128,8,128]{2,0,1:T(8,128)}, f32[128,8,128]{2,0,1:T(8,128)S(1)}, u32[]{:S(2)}, u32[]{:S(2)}) collective-permute-start(f32[128,8,128]{2,0,1:T(8,128)} %get-tuple-element.591), channel_id=1, source_target_pairs={{0,1},{1,2},{2,3},{3,4},{4,5},{5,6},{6,7},{7,8},{8,9},{9,10},{10,1... | collective-permute-start | bytes 1572872 | tf_op jit(solution)/shard_map/while/body/eval_jaxpr/ppermute | solution.py:96
  539.8 23.9 %collective-permute-start.3 = (f32[128,8,128]{2,0,1:T(8,128)}, f32[128,8,128]{2,0,1:T(8,128)S(1)}, u32[]{:S(2)}, u32[]{:S(2)}) collective-permute-start(f32[128,8,128]{2,0,1:T(8,128)} %get-tuple-element.592), channel_id=1, source_target_pairs={{0,1},{1,2},{2,3},{3,4},{4,5},{5,6},{6,7},{7,8},{8,9},{9,10},{10,1... | collective-permute-start | bytes 1572872 | tf_op jit(solution)/shard_map/while/body/eval_jaxpr/ppermute | solution.py:97
  539.8 23.9 %collective-permute-start.2 = (f32[128,8,128]{2,0,1:T(8,128)}, f32[128,8,128]{2,0,1:T(8,128)S(1)}, u32[]{:S(2)}, u32[]{:S(2)}) collective-permute-start(f32[128,8,128]{2,0,1:T(8,128)} %get-tuple-element.591), channel_id=1, source_target_pairs={{0,1},{1,2},{2,3},{3,4},{4,5},{5,6},{6,7},{7,8},{8,9},{9,10},{10,1... | collective-permute-start | bytes 1572872 | tf_op jit(solution)/shard_map/while/body/eval_jaxpr/ppermute | solution.py:96
  577.8 23.9 %collective-permute-start.3 = (f32[128,8,128]{2,0,1:T(8,128)}, f32[128,8,128]{2,0,1:T(8,128)S(1)}, u32[]{:S(2)}, u32[]{:S(2)}) collective-permute-start(f32[128,8,128]{2,0,1:T(8,128)} %get-tuple-element.592), channel_id=1, source_target_pairs={{0,1},{1,2},{2,3},{3,4},{4,5},{5,6},{6,7},{7,8},{8,9},{9,10},{10,1... | collective-permute-start | bytes 1572872 | tf_op jit(solution)/shard_map/while/body/eval_jaxpr/ppermute | solution.py:97
  577.8 23.9 %collective-permute-start.2 = (f32[128,8,128]{2,0,1:T(8,128)}, f32[128,8,128]{2,0,1:T(8,128)S(1)}, u32[]{:S(2)}, u32[]{:S(2)}) collective-permute-start(f32[128,8,128]{2,0,1:T(8,128)} %get-tuple-element.591), channel_id=1, source_target_pairs={{0,1},{1,2},{2,3},{3,4},{4,5},{5,6},{6,7},{7,8},{8,9},{9,10},{10,1... | collective-permute-start | bytes 1572872 | tf_op jit(solution)/shard_map/while/body/eval_jaxpr/ppermute | solution.py:96
  615.9 23.9 %collective-permute-start.3 = (f32[128,8,128]{2,0,1:T(8,128)}, f32[128,8,128]{2,0,1:T(8,128)S(1)}, u32[]{:S(2)}, u32[]{:S(2)}) collective-permute-start(f32[128,8,128]{2,0,1:T(8,128)} %get-tuple-element.592), channel_id=1, source_target_pairs={{0,1},{1,2},{2,3},{3,4},{4,5},{5,6},{6,7},{7,8},{8,9},{9,10},{10,1... | collective-permute-start | bytes 1572872 | tf_op jit(solution)/shard_map/while/body/eval_jaxpr/ppermute | solution.py:97
  615.9 23.9 %collective-permute-start.2 = (f32[128,8,128]{2,0,1:T(8,128)}, f32[128,8,128]{2,0,1:T(8,128)S(1)}, u32[]{:S(2)}, u32[]{:S(2)}) collective-permute-start(f32[128,8,128]{2,0,1:T(8,128)} %get-tuple-element.591), channel_id=1, source_target_pairs={{0,1},{1,2},{2,3},{3,4},{4,5},{5,6},{6,7},{7,8},{8,9},{9,10},{10,1... | collective-permute-start | bytes 1572872 | tf_op jit(solution)/shard_map/while/body/eval_jaxpr/ppermute | solution.py:96
  653.9 23.9 %collective-permute-start.3 = (f32[128,8,128]{2,0,1:T(8,128)}, f32[128,8,128]{2,0,1:T(8,128)S(1)}, u32[]{:S(2)}, u32[]{:S(2)}) collective-permute-start(f32[128,8,128]{2,0,1:T(8,128)} %get-tuple-element.592), channel_id=1, source_target_pairs={{0,1},{1,2},{2,3},{3,4},{4,5},{5,6},{6,7},{7,8},{8,9},{9,10},{10,1... | collective-permute-start | bytes 1572872 | tf_op jit(solution)/shard_map/while/body/eval_jaxpr/ppermute | solution.py:97
  653.9 23.9 %collective-permute-start.2 = (f32[128,8,128]{2,0,1:T(8,128)}, f32[128,8,128]{2,0,1:T(8,128)S(1)}, u32[]{:S(2)}, u32[]{:S(2)}) collective-permute-start(f32[128,8,128]{2,0,1:T(8,128)} %get-tuple-element.591), channel_id=1, source_target_pairs={{0,1},{1,2},{2,3},{3,4},{4,5},{5,6},{6,7},{7,8},{8,9},{9,10},{10,1... | collective-permute-start | bytes 1572872 | tf_op jit(solution)/shard_map/while/body/eval_jaxpr/ppermute | solution.py:96
  692.0 23.9 %collective-permute-start.3 = (f32[128,8,128]{2,0,1:T(8,128)}, f32[128,8,128]{2,0,1:T(8,128)S(1)}, u32[]{:S(2)}, u32[]{:S(2)}) collective-permute-start(f32[128,8,128]{2,0,1:T(8,128)} %get-tuple-element.592), channel_id=1, source_target_pairs={{0,1},{1,2},{2,3},{3,4},{4,5},{5,6},{6,7},{7,8},{8,9},{9,10},{10,1... | collective-permute-start | bytes 1572872 | tf_op jit(solution)/shard_map/while/body/eval_jaxpr/ppermute | solution.py:97
  692.0 23.9 %collective-permute-start.2 = (f32[128,8,128]{2,0,1:T(8,128)}, f32[128,8,128]{2,0,1:T(8,128)S(1)}, u32[]{:S(2)}, u32[]{:S(2)}) collective-permute-start(f32[128,8,128]{2,0,1:T(8,128)} %get-tuple-element.591), channel_id=1, source_target_pairs={{0,1},{1,2},{2,3},{3,4},{4,5},{5,6},{6,7},{7,8},{8,9},{9,10},{10,1... | collective-permute-start | bytes 1572872 | tf_op jit(solution)/shard_map/while/body/eval_jaxpr/ppermute | solution.py:96
  730.0 23.9 %collective-permute-start.3 = (f32[128,8,128]{2,0,1:T(8,128)}, f32[128,8,128]{2,0,1:T(8,128)S(1)}, u32[]{:S(2)}, u32[]{:S(2)}) collective-permute-start(f32[128,8,128]{2,0,1:T(8,128)} %get-tuple-element.592), channel_id=1, source_target_pairs={{0,1},{1,2},{2,3},{3,4},{4,5},{5,6},{6,7},{7,8},{8,9},{9,10},{10,1... | collective-permute-start | bytes 1572872 | tf_op jit(solution)/shard_map/while/body/eval_jaxpr/ppermute | solution.py:97
  730.0 23.9 %collective-permute-start.2 = (f32[128,8,128]{2,0,1:T(8,128)}, f32[128,8,128]{2,0,1:T(8,128)S(1)}, u32[]{:S(2)}, u32[]{:S(2)}) collective-permute-start(f32[128,8,128]{2,0,1:T(8,128)} %get-tuple-element.591), channel_id=1, source_target_pairs={{0,1},{1,2},{2,3},{3,4},{4,5},{5,6},{6,7},{7,8},{8,9},{9,10},{10,1... | collective-permute-start | bytes 1572872 | tf_op jit(solution)/shard_map/while/body/eval_jaxpr/ppermute | solution.py:96
  768.0 23.9 %collective-permute-start.3 = (f32[128,8,128]{2,0,1:T(8,128)}, f32[128,8,128]{2,0,1:T(8,128)S(1)}, u32[]{:S(2)}, u32[]{:S(2)}) collective-permute-start(f32[128,8,128]{2,0,1:T(8,128)} %get-tuple-element.592), channel_id=1, source_target_pairs={{0,1},{1,2},{2,3},{3,4},{4,5},{5,6},{6,7},{7,8},{8,9},{9,10},{10,1... | collective-permute-start | bytes 1572872 | tf_op jit(solution)/shard_map/while/body/eval_jaxpr/ppermute | solution.py:97
  768.0 23.9 %collective-permute-start.2 = (f32[128,8,128]{2,0,1:T(8,128)}, f32[128,8,128]{2,0,1:T(8,128)S(1)}, u32[]{:S(2)}, u32[]{:S(2)}) collective-permute-start(f32[128,8,128]{2,0,1:T(8,128)} %get-tuple-element.591), channel_id=1, source_target_pairs={{0,1},{1,2},{2,3},{3,4},{4,5},{5,6},{6,7},{7,8},{8,9},{9,10},{10,1... | collective-permute-start | bytes 1572872 | tf_op jit(solution)/shard_map/while/body/eval_jaxpr/ppermute | solution.py:96
  806.1 23.9 %collective-permute-start.3 = (f32[128,8,128]{2,0,1:T(8,128)}, f32[128,8,128]{2,0,1:T(8,128)S(1)}, u32[]{:S(2)}, u32[]{:S(2)}) collective-permute-start(f32[128,8,128]{2,0,1:T(8,128)} %get-tuple-element.592), channel_id=1, source_target_pairs={{0,1},{1,2},{2,3},{3,4},{4,5},{5,6},{6,7},{7,8},{8,9},{9,10},{10,1... | collective-permute-start | bytes 1572872 | tf_op jit(solution)/shard_map/while/body/eval_jaxpr/ppermute | solution.py:97
  806.1 23.9 %collective-permute-start.2 = (f32[128,8,128]{2,0,1:T(8,128)}, f32[128,8,128]{2,0,1:T(8,128)S(1)}, u32[]{:S(2)}, u32[]{:S(2)}) collective-permute-start(f32[128,8,128]{2,0,1:T(8,128)} %get-tuple-element.591), channel_id=1, source_target_pairs={{0,1},{1,2},{2,3},{3,4},{4,5},{5,6},{6,7},{7,8},{8,9},{9,10},{10,1... | collective-permute-start | bytes 1572872 | tf_op jit(solution)/shard_map/while/body/eval_jaxpr/ppermute | solution.py:96
  844.1 23.9 %collective-permute-start.3 = (f32[128,8,128]{2,0,1:T(8,128)}, f32[128,8,128]{2,0,1:T(8,128)S(1)}, u32[]{:S(2)}, u32[]{:S(2)}) collective-permute-start(f32[128,8,128]{2,0,1:T(8,128)} %get-tuple-element.592), channel_id=1, source_target_pairs={{0,1},{1,2},{2,3},{3,4},{4,5},{5,6},{6,7},{7,8},{8,9},{9,10},{10,1... | collective-permute-start | bytes 1572872 | tf_op jit(solution)/shard_map/while/body/eval_jaxpr/ppermute | solution.py:97
  844.1 23.9 %collective-permute-start.2 = (f32[128,8,128]{2,0,1:T(8,128)}, f32[128,8,128]{2,0,1:T(8,128)S(1)}, u32[]{:S(2)}, u32[]{:S(2)}) collective-permute-start(f32[128,8,128]{2,0,1:T(8,128)} %get-tuple-element.591), channel_id=1, source_target_pairs={{0,1},{1,2},{2,3},{3,4},{4,5},{5,6},{6,7},{7,8},{8,9},{9,10},{10,1... | collective-permute-start | bytes 1572872 | tf_op jit(solution)/shard_map/while/body/eval_jaxpr/ppermute | solution.py:96
  882.1 23.9 %collective-permute-start.3 = (f32[128,8,128]{2,0,1:T(8,128)}, f32[128,8,128]{2,0,1:T(8,128)S(1)}, u32[]{:S(2)}, u32[]{:S(2)}) collective-permute-start(f32[128,8,128]{2,0,1:T(8,128)} %get-tuple-element.592), channel_id=1, source_target_pairs={{0,1},{1,2},{2,3},{3,4},{4,5},{5,6},{6,7},{7,8},{8,9},{9,10},{10,1... | collective-permute-start | bytes 1572872 | tf_op jit(solution)/shard_map/while/body/eval_jaxpr/ppermute | solution.py:97
  882.1 23.9 %collective-permute-start.2 = (f32[128,8,128]{2,0,1:T(8,128)}, f32[128,8,128]{2,0,1:T(8,128)S(1)}, u32[]{:S(2)}, u32[]{:S(2)}) collective-permute-start(f32[128,8,128]{2,0,1:T(8,128)} %get-tuple-element.591), channel_id=1, source_target_pairs={{0,1},{1,2},{2,3},{3,4},{4,5},{5,6},{6,7},{7,8},{8,9},{9,10},{10,1... | collective-permute-start | bytes 1572872 | tf_op jit(solution)/shard_map/while/body/eval_jaxpr/ppermute | solution.py:96
  882.2 23.1 %collective-permute-start = (bf16[128,8,128]{2,0,1:T(8,128)(2,1)}, bf16[128,8,128]{2,0,1:T(8,128)(2,1)S(1)}, u32[]{:S(2)}, u32[]{:S(2)}) collective-permute-start(bf16[128,8,128]{2,0,1:T(8,128)(2,1)} %get-tuple-element.588), channel_id=1, source_target_pairs={{0,1},{1,2},{2,3},{3,4},{4,5},{5,6},{6,7},{7,8},{8,9},{9,10},{10,1... | collective-permute-start | bytes 786440 | tf_op jit(solution)/shard_map/while/body/eval_jaxpr/ppermute | solution.py:94
  920.2 23.9 %collective-permute-start.3 = (f32[128,8,128]{2,0,1:T(8,128)}, f32[128,8,128]{2,0,1:T(8,128)S(1)}, u32[]{:S(2)}, u32[]{:S(2)}) collective-permute-start(f32[128,8,128]{2,0,1:T(8,128)} %get-tuple-element.592), channel_id=1, source_target_pairs={{0,1},{1,2},{2,3},{3,4},{4,5},{5,6},{6,7},{7,8},{8,9},{9,10},{10,1... | collective-permute-start | bytes 1572872 | tf_op jit(solution)/shard_map/while/body/eval_jaxpr/ppermute | solution.py:97
  920.2 23.9 %collective-permute-start.2 = (f32[128,8,128]{2,0,1:T(8,128)}, f32[128,8,128]{2,0,1:T(8,128)S(1)}, u32[]{:S(2)}, u32[]{:S(2)}) collective-permute-start(f32[128,8,128]{2,0,1:T(8,128)} %get-tuple-element.591), channel_id=1, source_target_pairs={{0,1},{1,2},{2,3},{3,4},{4,5},{5,6},{6,7},{7,8},{8,9},{9,10},{10,1... | collective-permute-start | bytes 1572872 | tf_op jit(solution)/shard_map/while/body/eval_jaxpr/ppermute | solution.py:96
  958.2 23.9 %collective-permute-start.3 = (f32[128,8,128]{2,0,1:T(8,128)}, f32[128,8,128]{2,0,1:T(8,128)S(1)}, u32[]{:S(2)}, u32[]{:S(2)}) collective-permute-start(f32[128,8,128]{2,0,1:T(8,128)} %get-tuple-element.592), channel_id=1, source_target_pairs={{0,1},{1,2},{2,3},{3,4},{4,5},{5,6},{6,7},{7,8},{8,9},{9,10},{10,1... | collective-permute-start | bytes 1572872 | tf_op jit(solution)/shard_map/while/body/eval_jaxpr/ppermute | solution.py:97
  958.2 23.9 %collective-permute-start.2 = (f32[128,8,128]{2,0,1:T(8,128)}, f32[128,8,128]{2,0,1:T(8,128)S(1)}, u32[]{:S(2)}, u32[]{:S(2)}) collective-permute-start(f32[128,8,128]{2,0,1:T(8,128)} %get-tuple-element.591), channel_id=1, source_target_pairs={{0,1},{1,2},{2,3},{3,4},{4,5},{5,6},{6,7},{7,8},{8,9},{9,10},{10,1... | collective-permute-start | bytes 1572872 | tf_op jit(solution)/shard_map/while/body/eval_jaxpr/ppermute | solution.py:96
  996.3 23.9 %collective-permute-start.3 = (f32[128,8,128]{2,0,1:T(8,128)}, f32[128,8,128]{2,0,1:T(8,128)S(1)}, u32[]{:S(2)}, u32[]{:S(2)}) collective-permute-start(f32[128,8,128]{2,0,1:T(8,128)} %get-tuple-element.592), channel_id=1, source_target_pairs={{0,1},{1,2},{2,3},{3,4},{4,5},{5,6},{6,7},{7,8},{8,9},{9,10},{10,1... | collective-permute-start | bytes 1572872 | tf_op jit(solution)/shard_map/while/body/eval_jaxpr/ppermute | solution.py:97
  996.3 23.9 %collective-permute-start.2 = (f32[128,8,128]{2,0,1:T(8,128)}, f32[128,8,128]{2,0,1:T(8,128)S(1)}, u32[]{:S(2)}, u32[]{:S(2)}) collective-permute-start(f32[128,8,128]{2,0,1:T(8,128)} %get-tuple-element.591), channel_id=1, source_target_pairs={{0,1},{1,2},{2,3},{3,4},{4,5},{5,6},{6,7},{7,8},{8,9},{9,10},{10,1... | collective-permute-start | bytes 1572872 | tf_op jit(solution)/shard_map/while/body/eval_jaxpr/ppermute | solution.py:96
  1034.3 23.9 %collective-permute-start.3 = (f32[128,8,128]{2,0,1:T(8,128)}, f32[128,8,128]{2,0,1:T(8,128)S(1)}, u32[]{:S(2)}, u32[]{:S(2)}) collective-permute-start(f32[128,8,128]{2,0,1:T(8,128)} %get-tuple-element.592), channel_id=1, source_target_pairs={{0,1},{1,2},{2,3},{3,4},{4,5},{5,6},{6,7},{7,8},{8,9},{9,10},{10,1... | collective-permute-start | bytes 1572872 | tf_op jit(solution)/shard_map/while/body/eval_jaxpr/ppermute | solution.py:97
  1034.3 23.9 %collective-permute-start.2 = (f32[128,8,128]{2,0,1:T(8,128)}, f32[128,8,128]{2,0,1:T(8,128)S(1)}, u32[]{:S(2)}, u32[]{:S(2)}) collective-permute-start(f32[128,8,128]{2,0,1:T(8,128)} %get-tuple-element.591), channel_id=1, source_target_pairs={{0,1},{1,2},{2,3},{3,4},{4,5},{5,6},{6,7},{7,8},{8,9},{9,10},{10,1... | collective-permute-start | bytes 1572872 | tf_op jit(solution)/shard_map/while/body/eval_jaxpr/ppermute | solution.py:96
  1034.3 23.1 %collective-permute-start = (bf16[128,8,128]{2,0,1:T(8,128)(2,1)}, bf16[128,8,128]{2,0,1:T(8,128)(2,1)S(1)}, u32[]{:S(2)}, u32[]{:S(2)}) collective-permute-start(bf16[128,8,128]{2,0,1:T(8,128)(2,1)} %get-tuple-element.588), channel_id=1, source_target_pairs={{0,1},{1,2},{2,3},{3,4},{4,5},{5,6},{6,7},{7,8},{8,9},{9,10},{10,1... | collective-permute-start | bytes 786440 | tf_op jit(solution)/shard_map/while/body/eval_jaxpr/ppermute | solution.py:94
  1072.3 23.9 %collective-permute-start.3 = (f32[128,8,128]{2,0,1:T(8,128)}, f32[128,8,128]{2,0,1:T(8,128)S(1)}, u32[]{:S(2)}, u32[]{:S(2)}) collective-permute-start(f32[128,8,128]{2,0,1:T(8,128)} %get-tuple-element.592), channel_id=1, source_target_pairs={{0,1},{1,2},{2,3},{3,4},{4,5},{5,6},{6,7},{7,8},{8,9},{9,10},{10,1... | collective-permute-start | bytes 1572872 | tf_op jit(solution)/shard_map/while/body/eval_jaxpr/ppermute | solution.py:97
  1072.3 23.9 %collective-permute-start.2 = (f32[128,8,128]{2,0,1:T(8,128)}, f32[128,8,128]{2,0,1:T(8,128)S(1)}, u32[]{:S(2)}, u32[]{:S(2)}) collective-permute-start(f32[128,8,128]{2,0,1:T(8,128)} %get-tuple-element.591), channel_id=1, source_target_pairs={{0,1},{1,2},{2,3},{3,4},{4,5},{5,6},{6,7},{7,8},{8,9},{9,10},{10,1... | collective-permute-start | bytes 1572872 | tf_op jit(solution)/shard_map/while/body/eval_jaxpr/ppermute | solution.py:96
  1110.4 23.9 %collective-permute-start.3 = (f32[128,8,128]{2,0,1:T(8,128)}, f32[128,8,128]{2,0,1:T(8,128)S(1)}, u32[]{:S(2)}, u32[]{:S(2)}) collective-permute-start(f32[128,8,128]{2,0,1:T(8,128)} %get-tuple-element.592), channel_id=1, source_target_pairs={{0,1},{1,2},{2,3},{3,4},{4,5},{5,6},{6,7},{7,8},{8,9},{9,10},{10,1... | collective-permute-start | bytes 1572872 | tf_op jit(solution)/shard_map/while/body/eval_jaxpr/ppermute | solution.py:97
  1110.4 23.9 %collective-permute-start.2 = (f32[128,8,128]{2,0,1:T(8,128)}, f32[128,8,128]{2,0,1:T(8,128)S(1)}, u32[]{:S(2)}, u32[]{:S(2)}) collective-permute-start(f32[128,8,128]{2,0,1:T(8,128)} %get-tuple-element.591), channel_id=1, source_target_pairs={{0,1},{1,2},{2,3},{3,4},{4,5},{5,6},{6,7},{7,8},{8,9},{9,10},{10,1... | collective-permute-start | bytes 1572872 | tf_op jit(solution)/shard_map/while/body/eval_jaxpr/ppermute | solution.py:96
  1148.4 23.9 %collective-permute-start.3 = (f32[128,8,128]{2,0,1:T(8,128)}, f32[128,8,128]{2,0,1:T(8,128)S(1)}, u32[]{:S(2)}, u32[]{:S(2)}) collective-permute-start(f32[128,8,128]{2,0,1:T(8,128)} %get-tuple-element.592), channel_id=1, source_target_pairs={{0,1},{1,2},{2,3},{3,4},{4,5},{5,6},{6,7},{7,8},{8,9},{9,10},{10,1... | collective-permute-start | bytes 1572872 | tf_op jit(solution)/shard_map/while/body/eval_jaxpr/ppermute | solution.py:97
  1148.4 23.9 %collective-permute-start.2 = (f32[128,8,128]{2,0,1:T(8,128)}, f32[128,8,128]{2,0,1:T(8,128)S(1)}, u32[]{:S(2)}, u32[]{:S(2)}) collective-permute-start(f32[128,8,128]{2,0,1:T(8,128)} %get-tuple-element.591), channel_id=1, source_target_pairs={{0,1},{1,2},{2,3},{3,4},{4,5},{5,6},{6,7},{7,8},{8,9},{9,10},{10,1... | collective-permute-start | bytes 1572872 | tf_op jit(solution)/shard_map/while/body/eval_jaxpr/ppermute | solution.py:96
  1186.4 23.9 %collective-permute-start.3 = (f32[128,8,128]{2,0,1:T(8,128)}, f32[128,8,128]{2,0,1:T(8,128)S(1)}, u32[]{:S(2)}, u32[]{:S(2)}) collective-permute-start(f32[128,8,128]{2,0,1:T(8,128)} %get-tuple-element.592), channel_id=1, source_target_pairs={{0,1},{1,2},{2,3},{3,4},{4,5},{5,6},{6,7},{7,8},{8,9},{9,10},{10,1... | collective-permute-start | bytes 1572872 | tf_op jit(solution)/shard_map/while/body/eval_jaxpr/ppermute | solution.py:97
  1186.5 23.9 %collective-permute-start.2 = (f32[128,8,128]{2,0,1:T(8,128)}, f32[128,8,128]{2,0,1:T(8,128)S(1)}, u32[]{:S(2)}, u32[]{:S(2)}) collective-permute-start(f32[128,8,128]{2,0,1:T(8,128)} %get-tuple-element.591), channel_id=1, source_target_pairs={{0,1},{1,2},{2,3},{3,4},{4,5},{5,6},{6,7},{7,8},{8,9},{9,10},{10,1... | collective-permute-start | bytes 1572872 | tf_op jit(solution)/shard_map/while/body/eval_jaxpr/ppermute | solution.py:96
  (187 other events, 1584.4 us)
where the time goes:
time: 1330 us; the launch traced here: 1320 us
  waiting for transfers between devices  637 us (48%)
  local copies, waits for them, and re-layouts  317 us (24%)
  matrix products  228 us (17%)
  blocking collectives  65.6 us (5%)
  other arithmetic  47.6 us (4%)
  starting transfers between devices  16.3 us (1%)
    ppermute x31, waiting for transfers between devices, visit_source(): v_cur = lax.ppermute(v_cur, 'cp', shift_pairs)  634 us
    another operation x60, local copies, waits for them, and re-layouts  152 us
    while x124, local copies, waits for them, and re-layouts  98.5 us
    dot_general x34, matrix products, pair_grads(): jnp.einsum('qngd,knd->qngk', do_blk, v_blk, preferred_element_type=jnp.fl...  90.7 us
    dot_general x34, matrix products, pair_grads(): jnp.einsum('qngk,qngd->knd', prob_bf, do_blk, preferred_element_type=jnp....  68.3 us
    psum x1, blocking collectives, local_grads(): lax.psum(dq_weight, 'cp')  65.6 us
    cond x126, local copies, waits for them, and re-layouts  33.7 us
    dot_general x34, matrix products, pair_grads(): jnp.einsum('qngk,knd->qngd', score_grad, k_blk, preferred_element_type=jn...  31.7 us
  transfers between devices with their start and end apart: 126, of which 35 were waited for; matrix products, arithmetic and copies ran while one was open for 7% of the time, Pallas kernels for 0%

commit v1 on v0

v1 whole, which is shorter than its diff:
```python
import functools
import math

import jax
import jax.numpy as jnp
from jax import lax
from jax.experimental import pallas as pl
from jax.experimental.pallas import tpu as pltpu
from jax.sharding import PartitionSpec as P

HEAD_DIM = 128
ROPE_THETA = 1000000.0
NORM_EPS = 1e-6
SM_SCALE = HEAD_DIM ** -0.5
LOG2E = math.log2(math.e)
F32, BF16 = jnp.float32, jnp.bfloat16
NN = (((1,), (0,)), ((), ()))
NT = (((1,), (1,)), ((), ()))
SUB = 16


def rope_tables(positions):
    inv_freq = ROPE_THETA ** (-jnp.arange(0, HEAD_DIM, 2).astype(F32) / HEAD_DIM)
    angles = positions.astype(F32)[:, None] * inv_freq[None, :]
    angles = jnp.concatenate([angles, angles], axis=-1)
    return jnp.cos(angles), jnp.sin(angles)


def norm_rope(raw_in, weight, cos_t, sin_t):
    mean_sq = jnp.mean(raw_in * raw_in, axis=-1, keepdims=True)
    normed = raw_in * lax.rsqrt(mean_sq + NORM_EPS) * weight
    half_dim = raw_in.shape[-1] // 2
    rotated = jnp.concatenate([-normed[..., half_dim:], normed[..., :half_dim]], axis=-1)
    return normed * cos_t + rotated * sin_t


def dot(a, b, dims):
    return lax.dot_general(a, b, dims, preferred_element_type=F32)


def kernel(side, chunk, per_kv, q_hbm, do_hbm, kv_hbm, st_hbm, cos_ref, sin_ref, qn_ref, kn_ref,
           dq_hbm, dkv_hbm, dw_ref,
           qbuf, dobuf, kbuf, stbuf, q_s, do_s, qT, doT, lc, dc, acc, rsbuf, dq_acc, dqo, dko, dwq, dwk, xbuf,
           in_send, kv_send, kv_recv, st_recv, q_recv, do_recv, ag_send, ag_recv, rs_send, rs_recv,
           dq_send, dq_recv, dk_send, dk_recv, x_send, x_recv):
    me = lax.axis_index('cp')
    core = lax.rem(me, 2)
    chip = me // 2
    x = lax.rem(chip, side)
    y = chip // side
    a = (1 - core) * x + core * y
    b = (1 - core) * y + core * x
    head = core * side + a
    top = 2 * side - 1
    rows = 2 * chunk * per_kv
    tile = side * 2 * chunk

    def role_dev(role, ra, rb):
        return ((1 - role) * (rb * side + ra) + role * (ra * side + rb)) * 2 + role

    def dev(d):
        return {'cp': d}

    def remote(src, dst, ssem, rsem, d):
        return pltpu.make_async_remote_copy(src_ref=src, dst_ref=dst, send_sem=ssem, recv_sem=rsem,
                                            device_id=dev(d), device_id_type=pl.DeviceIdType.MESH)

    def landed(ref, sem):
        pltpu.make_async_copy(ref, ref, sem).wait()

    barrier = pltpu.get_barrier_semaphore()
    for dx in range(side):
        for cc in range(2):
            in_row = (y * side + lax.rem(x + dx, side)) * 2 + cc
            in_col = (lax.rem(y + dx, side) * side + x) * 2 + cc
            if dx == 0:
                if cc == 0:
                    pl.semaphore_signal(barrier, inc=1, device_id=dev(chip * 2 + 1 - core), device_id_type=pl.DeviceIdType.MESH)
            else:
                pl.semaphore_signal(barrier, inc=1, device_id=dev(in_row), device_id_type=pl.DeviceIdType.MESH)
                pl.semaphore_signal(barrier, inc=1, device_id=dev(in_col), device_id_type=pl.DeviceIdType.MESH)
    pl.semaphore_wait(barrier, 4 * (side - 1) + 1)

    def in_copies(role, ra, slot):
        hd = role * side + ra
        group = pl.ds(pl.multiple_of(hd * per_kv, per_kv), per_kv)
        kv = []
        for lohi in range(2):
            jj = y if lohi == 0 else top - y
            ii = x if lohi == 0 else side - 1 - x
            half = core if lohi == 0 else 1 - core
            kv.append((kv_hbm.at[hd, lohi], kbuf.at[jj, ii, half], kv_send.at[lohi, role, ra], kv_recv.at[lohi, slot, core]))
        return kv + [(st_hbm.at[hd], stbuf.at[slot, core], in_send.at[0, role, ra], st_recv.at[slot, core]),
                     (q_hbm.at[:, group, :], qbuf.at[slot, core], in_send.at[1, role, ra], q_recv.at[slot, core]),
                     (do_hbm.at[:, group, :], dobuf.at[slot, core], in_send.at[2, role, ra], do_recv.at[slot, core])]

    def coord(role):
        return x if role == 0 else y

    def targets():
        part = 1 - core
        part_a = (1 - part) * x + part * y
        yield part, part_a, part_a, chip * 2 + part
        for dx in (1, side - 1) + tuple(range(2, side - 1)):
            for role in range(2):
                ra = lax.rem(coord(role) + dx, side)
                yield role, ra, coord(role), role_dev(role, ra, y if role == 0 else x)

    own = in_copies(core, a, a)
    sends = []
    for role, ra, slot, d in targets():
        sends.append([remote(s, t, ss, rs, d) for s, t, ss, rs in in_copies(role, ra, slot)])
    for which in ((0, 1), (2, 3, 4)):
        for n in which:
            pltpu.make_async_copy(own[n][0], own[n][1], own[n][3]).start()
        for group in sends:
            for n in which:
                group[n].start()

    acc[...] = jnp.zeros_like(acc)
    dq_acc[...] = jnp.zeros_like(dq_acc)
    dwq[...] = jnp.zeros_like(dwq)
    dwk[...] = jnp.zeros_like(dwk)

    def place(lohi, s, bb):
        ys, xs = (1 - core) * bb + core * s, (1 - core) * s + core * bb
        return (ys, xs) if lohi == 0 else (top - ys, side - 1 - xs)

    ag = []
    for ds in range(side):
        s = lax.rem(a + ds, side)
        for lohi in range(2):
            jj, ii = place(lohi, s, b)
            for cc in range(2):
                landed(kbuf.at[jj, ii, cc], kv_recv.at[lohi, s, cc])
            piece = kbuf.at[jj, ii, :, pl.ds(0, 2)]
            for db in range(1, side):
                cp = remote(piece, piece, ag_send.at[db, lohi, s], ag_recv.at[b, lohi, s],
                            role_dev(core, a, lax.rem(b + db, side)))
                cp.start()
                ag.append(cp)

    def piece_owner(j, i):
        hi = j // side
        jj = j + hi * (top - 2 * j)
        ii = i + hi * (side - 1 - 2 * i)
        return hi, (1 - core) * jj + core * ii, (1 - core) * ii + core * jj

    def block_index(s, lohi):
        cc = (1 - core) * (b * side + s) + core * (s * side + b)
        return cc + lohi * (2 * side * side - 1 - 2 * cc)

    def rope_rows(tref, s, cs, lohi, r0):
        t = tref[s, cs, lohi, pl.ds(r0, SUB), :]
        return jnp.broadcast_to(t[:, None, :], (SUB, per_kv, HEAD_DIM)).reshape(SUB * per_kv, HEAD_DIM)

    def steps(fn):
        n = chunk // SUB

        def body(t, _):
            fn(t, t // n, lax.rem(t, n))
            return 0
        lax.fori_loop(0, 2 * n, body, 0)

    step_rows = SUB * per_kv

    def prepare(s, lohi):
        bi = s * 2 + lohi

        def one(t, cs, sub):
            r0 = pl.multiple_of(sub * SUB, SUB)
            src = pl.ds(pl.multiple_of(lohi * chunk + sub * SUB, SUB), SUB)
            dst = pl.ds(pl.multiple_of(t * step_rows, step_rows), step_rows)
            xq = qbuf[s, cs, src].astype(F32).reshape(step_rows, HEAD_DIM)
            ms = jnp.mean(xq * xq, axis=-1, keepdims=True)
            nq = xq * lax.rsqrt(ms + NORM_EPS) * qn_ref[...]
            qf = nq * rope_rows(cos_ref, s, cs, lohi, r0) + pltpu.roll(nq, HEAD_DIM // 2, 1) * rope_rows(sin_ref, s, cs, lohi, r0)
            q_s[bi, dst, :] = qf.astype(BF16)
            qT[bi, :, dst] = qf.T.astype(BF16)
            dof = dobuf[s, cs, src].astype(F32).reshape(step_rows, HEAD_DIM)
            do_s[bi, dst, :] = dof.astype(BF16)
            doT[bi, :, dst] = dof.T.astype(BF16)
            lanes = pl.ds(pl.multiple_of(sub * step_rows, step_rows), step_rows)
            lc[bi, dst, :] = jnp.broadcast_to(stbuf[s, cs, pl.ds(lohi, 1), lanes], (HEAD_DIM, step_rows)).T
            dc[bi, dst, :] = jnp.broadcast_to(stbuf[s, cs, pl.ds(2 + lohi, 1), lanes], (HEAD_DIM, step_rows)).T
        steps(one)

    def norm_back(g, xr, w, cos_t, sin_t):
        ms = jnp.mean(xr * xr, axis=-1, keepdims=True)
        r = lax.rsqrt(ms + NORM_EPS)
        dn = g * cos_t - pltpu.roll(g, HEAD_DIM // 2, 1) * sin_t
        xh = xr * r
        t = dn * w
        dx = r * (t - xh * jnp.mean(t * xh, axis=-1, keepdims=True))
        return dx, dn * xh

    def finish(s, lohi):
        bi = s * 2 + lohi

        def one(t, cs, sub):
            r0 = pl.multiple_of(sub * SUB, SUB)
            src = pl.ds(pl.multiple_of(lohi * chunk + sub * SUB, SUB), SUB)
            dst = pl.ds(pl.multiple_of(t * step_rows, step_rows), step_rows)
            xq = qbuf[s, cs, src].astype(F32).reshape(step_rows, HEAD_DIM)
            dx, dwt = norm_back(dq_acc[bi, dst, :] * SM_SCALE, xq, qn_ref[...],
                                rope_rows(cos_ref, s, cs, lohi, r0), rope_rows(sin_ref, s, cs, lohi, r0))
            dwq[...] += jnp.sum(dwt.reshape(SUB, 8, HEAD_DIM) if per_kv == 8 else dwt.reshape(step_rows // 8, 8, HEAD_DIM), axis=0)
            dqo[s, cs, src] = dx.reshape(SUB, per_kv, HEAD_DIM).astype(BF16)
        steps(one)
        for cs in range(2):
            part = pl.ds(pl.multiple_of(lohi * chunk, chunk), chunk)
            src = dqo.at[s, cs, part]
            dst = dq_hbm.at[part, pl.ds(pl.multiple_of(head * per_kv, per_kv), per_kv), :]
            target = ((1 - core) * (b * side + s) + core * (s * side + b)) * 2 + cs
            mine = target == me

            @pl.when(mine)
            def _():
                pltpu.make_async_copy(src, dst, dq_recv.at[head, lohi]).start()

            @pl.when(jnp.logical_not(mine))
            def _():
                remote(src, dst, dq_send.at[s, cs, lohi], dq_recv.at[head, lohi], target).start()

    def compute(s, lohi, j, masked):
        bi = s * 2 + lohi
        kt = kbuf[j, :, :, 0].reshape(tile, HEAD_DIM)
        vt = kbuf[j, :, :, 1].reshape(tile, HEAD_DIM)
        z = dot(q_s[bi], kt, NT) * (SM_SCALE * LOG2E) - jnp.tile(lc[bi], (1, tile // HEAD_DIM))
        if masked:
            first = block_index(s, lohi)
            row = lax.broadcasted_iota(jnp.int32, (rows, tile), 0) // per_kv
            half, off = row // chunk, lax.rem(row, chunk)
            half = half + lohi * (1 - 2 * half)
            q_pos = first * (2 * chunk) + half * chunk + off
            k_pos = lax.broadcasted_iota(jnp.int32, (rows, tile), 1) + j * tile
            z = jnp.where(k_pos <= q_pos, z, -jnp.inf)
        p = jnp.exp2(z)
        dp = dot(do_s[bi], vt, NT)
        ds = (p * (dp - jnp.tile(dc[bi], (1, tile // HEAD_DIM)))).astype(BF16)
        pb = p.astype(BF16)
        dv_t = dot(doT[bi], pb, NN)
        dk_t = dot(qT[bi], ds, NN)
        for i in range(side):
            cols = slice(i * 2 * chunk, (i + 1) * 2 * chunk)
            acc[j, i, 0] += dk_t[:, cols]
            acc[j, i, 1] += dv_t[:, cols]
        dq_acc[bi] += dot(ds, kt, NN)

    def rs_copy(j, i, lohi, ob, os):
        return remote(acc.at[j, i], rsbuf.at[b, lohi, os], rs_send.at[j, i], rs_recv.at[b, lohi, os], role_dev(core, a, ob))

    n_group = 2
    per_group = side // n_group

    def group_slot(grp, k):
        n = grp * per_group + k
        return lax.rem(a + n, side)

    def group_body(grp, _):
        def prep_body(k, _):
            s = group_slot(grp, k)
            for cs in range(2):
                landed(stbuf.at[s, cs], st_recv.at[s, cs])
                landed(qbuf.at[s, cs], q_recv.at[s, cs])
                landed(dobuf.at[s, cs], do_recv.at[s, cs])
            prepare(s, 0)
            prepare(s, 1)
            return 0
        lax.fori_loop(0, per_group, prep_body, 0)

        def tile_body(j, _):
            @pl.when(grp == 0)
            def _():
                for i in range(side):
                    lohi, ob, os = piece_owner(j, i)

                    @pl.when(ob != b)
                    def _():
                        landed(kbuf.at[j, i, :, pl.ds(0, 2)], ag_recv.at[ob, lohi, os])

            def block_body(k, _):
                s, lohi = group_slot(grp, k // 2), lax.rem(k, 2)
                full = block_index(s, lohi) // side

                @pl.when(j < full)
                def _():
                    compute(s, lohi, j, False)

                @pl.when(j == full)
                def _():
                    compute(s, lohi, j, True)
                    finish(s, lohi)
                return 0
            lax.fori_loop(0, 2 * per_group, block_body, 0)

            @pl.when(grp == n_group - 1)
            def _():
                for i in range(side):
                    lohi, ob, os = piece_owner(j, i)

                    @pl.when(ob != b)
                    def _():
                        rs_copy(j, i, lohi, ob, os).start()
            return 0
        lax.fori_loop(0, 2 * side, tile_body, 0)
        return 0
    lax.fori_loop(0, n_group, group_body, 0)

    def own_body(t, _):
        lohi, s = t // side, lax.rem(t, side)
        ys, xs = (1 - core) * b + core * s, (1 - core) * s + core * b
        jj = ys + lohi * (top - 2 * ys)
        ii = xs + lohi * (side - 1 - 2 * xs)
        for db in range(1, side):
            ob = lax.rem(b + db, side)
            landed(rsbuf.at[ob, lohi, s], rs_recv.at[ob, lohi, s])
        total = [acc[jj, ii, n] for n in range(2)]
        for db in range(1, side):
            ob = lax.rem(b + db, side)
            total = [total[n] + rsbuf[ob, lohi, s, n] for n in range(2)]
        dk, dv = total[0].T * SM_SCALE, total[1].T
        for half in range(2):
            cs = half + lohi * (1 - 2 * half)
            part = slice(half * chunk, (half + 1) * chunk)
            kr = kbuf[jj, ii, half, 2].astype(F32)
            dx, dwt = norm_back(dk[part], kr, kn_ref[...], cos_ref[s, cs, lohi], sin_ref[s, cs, lohi])
            dwk[...] += jnp.sum(dwt.reshape(chunk // 8, 8, HEAD_DIM), axis=0)
            dko[lohi, s, half, 0] = dx.astype(BF16)
            dko[lohi, s, half, 1] = dv[part].astype(BF16)
            target = ((1 - core) * (b * side + s) + core * (s * side + b)) * 2 + cs
            src, dst = dko.at[lohi, s, half], dkv_hbm.at[head, lohi]
            mine = target == me

            @pl.when(mine)
            def _():
                pltpu.make_async_copy(src, dst, dk_recv.at[head, lohi]).start()

            @pl.when(jnp.logical_not(mine))
            def _():
                remote(src, dst, dk_send.at[lohi, s, half], dk_recv.at[head, lohi], target).start()
        return 0
    lax.fori_loop(0, 2 * side, own_body, 0)

    xbuf[0, a, 0] = dwq[...]
    xbuf[0, a, 1] = dwk[...]
    for stage in range(2):
        pos = (a, b)[stage]
        cps = []
        for d in range(1, side):
            o = lax.rem(pos + d, side)
            other = role_dev(core, o, b) if stage == 0 else role_dev(core, a, o)
            cp = remote(xbuf.at[stage, pos], xbuf.at[stage, pos], x_send.at[stage, d], x_recv.at[stage, pos], other)
            cp.start()
            cps.append(cp)
        for d in range(1, side):
            o = lax.rem(pos + d, side)
            landed(xbuf.at[stage, o], x_recv.at[stage, o])
        total = xbuf[stage, 0]
        for o in range(1, side):
            total = total + xbuf[stage, o]
        for cp in cps:
            cp.wait_send()
        if stage == 0:
            xbuf[1, b] = total
        else:
            xbuf[2, core] = total
    cp = remote(xbuf.at[2, core], xbuf.at[2, core], x_send.at[2, 0], x_recv.at[2, core], chip * 2 + 1 - core)
    cp.start()
    landed(xbuf.at[2, 1 - core], x_recv.at[2, 1 - core])
    dw_ref[...] = xbuf[2, 0] + xbuf[2, 1]
    cp.wait_send()

    for group in sends:
        for cp in group:
            cp.wait_send()
    for cp in ag:
        cp.wait_send()

    def drain_rs(j, _):
        for i in range(side):
            lohi, ob, os = piece_owner(j, i)

            @pl.when(ob != b)
            def _():
                rs_copy(j, i, lohi, ob, os).wait_send()
        return 0
    lax.fori_loop(0, 2 * side, drain_rs, 0)

    def drain_out(t, _):
        s, lohi = t // 2, lax.rem(t, 2)
        for cs in range(2):
            target = ((1 - core) * (b * side + s) + core * (s * side + b)) * 2 + cs
            half = cs + lohi * (1 - 2 * cs)

            @pl.when(target != me)
            def _():
                part = dqo.at[s, cs, pl.ds(0, chunk)]
                pltpu.make_async_copy(part, part, dq_send.at[s, cs, lohi]).wait()
                part = dko.at[lohi, s, half]
                pltpu.make_async_copy(part, part, dk_send.at[lohi, s, half]).wait()
        return 0
    lax.fori_loop(0, 2 * side, drain_out, 0)

    def drain_in(t, _):
        hd, lohi = t // 2, lax.rem(t, 2)
        part = pl.ds(pl.multiple_of(lohi * chunk, chunk), chunk)
        landed(dq_hbm.at[part, pl.ds(pl.multiple_of(hd * per_kv, per_kv), per_kv), :], dq_recv.at[hd, lohi])
        landed(dkv_hbm.at[hd, lohi], dk_recv.at[hd, lohi])
        return 0
    lax.fori_loop(0, 4 * side, drain_in, 0)


def solution(mesh):
    cp_size = mesh.shape['cp']
    side = math.isqrt(cp_size // 2)

    def local_grads(q_raw, k_raw, v_proj, out_fwd, lse_fwd, d_out, q_norm, k_norm):
        me = lax.axis_index('cp')
        local_rows, num_heads = q_raw.shape[0], q_raw.shape[1]
        chunk = local_rows // 2
        kv_heads = k_raw.shape[1]
        per_kv = num_heads // kv_heads
        core, chip = me % 2, me // 2
        x, y = chip % side, chip // side

        offs = jnp.arange(chunk)

        def chunk_positions(device):
            return jnp.stack([device * chunk + offs, (2 * cp_size - 1 - device) * chunk + offs], axis=-2)

        cos_k, sin_k = rope_tables(chunk_positions(me).reshape(-1))
        k_b = norm_rope(k_raw.astype(F32), k_norm, cos_k[:, None, :], sin_k[:, None, :]).astype(BF16)
        kv = jnp.stack([k_b, v_proj, k_raw]).reshape(3, 2, chunk, kv_heads, HEAD_DIM).transpose(3, 1, 0, 2, 4)
        delta = jnp.sum(d_out.astype(F32) * out_fwd.astype(F32), axis=-1)
        stats = jnp.stack([lse_fwd * LOG2E, delta]).reshape(2, 2, chunk, kv_heads, per_kv)
        stats = stats.transpose(3, 0, 1, 2, 4).reshape(kv_heads, 4, chunk * per_kv)

        slots = jnp.arange(side)
        src_chip = jnp.where(core == 0, y * side + slots, slots * side + x)
        src_dev = src_chip[:, None] * 2 + jnp.arange(2)[None, :]
        pos = chunk_positions(src_dev[:, :, None, None])
        cos_t, sin_t = rope_tables(pos.reshape(-1))
        sign = jnp.where(jnp.arange(HEAD_DIM) < HEAD_DIM // 2, -1.0, 1.0).astype(F32)
        cos_t = cos_t.reshape(side, 2, 2, chunk, HEAD_DIM)
        sin_t = (sin_t * sign).reshape(side, 2, 2, chunk, HEAD_DIM)

        rows = local_rows * per_kv
        dma = pltpu.SemaphoreType.DMA
        any_spec, vmem_spec = pl.BlockSpec(memory_space=pl.ANY), pl.BlockSpec(memory_space=pltpu.VMEM)
        dq_raw, dkv, dw = pl.pallas_call(
            functools.partial(kernel, side, chunk, per_kv),
            out_shape=(jax.ShapeDtypeStruct(q_raw.shape, BF16),
                       jax.ShapeDtypeStruct((kv_heads, 2, 2, chunk, HEAD_DIM), BF16),
                       jax.ShapeDtypeStruct((2, 8, HEAD_DIM), F32)),
            in_specs=[any_spec] * 4 + [vmem_spec] * 4,
            out_specs=(any_spec, any_spec, vmem_spec),
            scratch_shapes=[
                pltpu.VMEM((side, 2, local_rows, per_kv, HEAD_DIM), BF16),
                pltpu.VMEM((side, 2, local_rows, per_kv, HEAD_DIM), BF16),
                pltpu.VMEM((2 * side, side, 2, 3, chunk, HEAD_DIM), BF16),
                pltpu.VMEM((side, 2, 4, chunk * per_kv), F32),
                pltpu.VMEM((2 * side, rows, HEAD_DIM), BF16),
                pltpu.VMEM((2 * side, rows, HEAD_DIM), BF16),
                pltpu.VMEM((2 * side, HEAD_DIM, rows), BF16),
                pltpu.VMEM((2 * side, HEAD_DIM, rows), BF16),
                pltpu.VMEM((2 * side, rows, HEAD_DIM), F32),
                pltpu.VMEM((2 * side, rows, HEAD_DIM), F32),
                pltpu.VMEM((2 * side, side, 2, HEAD_DIM, 2 * chunk), F32),
                pltpu.VMEM((side, 2, side, 2, HEAD_DIM, 2 * chunk), F32),
                pltpu.VMEM((2 * side, rows, HEAD_DIM), F32),
                pltpu.VMEM((side, 2, local_rows, per_kv, HEAD_DIM), BF16),
                pltpu.VMEM((2, side, 2, 2, chunk, HEAD_DIM), BF16),
                pltpu.VMEM((8, HEAD_DIM), F32),
                pltpu.VMEM((8, HEAD_DIM), F32),
                pltpu.VMEM((3, side, 2, 8, HEAD_DIM), F32),
                dma((3, 2, side)), dma((2, 2, side)), dma((2, side, 2)), dma((side, 2)), dma((side, 2)), dma((side, 2)),
                dma((side, 2, side)), dma((side, 2, side)), dma((2 * side, side)), dma((side, 2, side)),
                dma((side, 2, 2)), dma((kv_heads, 2)), dma((2, side, 2)), dma((kv_heads, 2)),
                dma((3, side)), dma((3, side)),
            ],
            compiler_params=pltpu.CompilerParams(collective_id=0, has_side_effects=True, vmem_limit_bytes=60 << 20),
            name='attention_backward',
        )(q_raw, d_out, kv, stats, cos_t, sin_t, q_norm[None, :], k_norm[None, :])
        dkv = dkv.transpose(2, 1, 3, 0, 4).reshape(2, local_rows, kv_heads, HEAD_DIM)
        dw = jnp.sum(dw, axis=1)
        return dq_raw, dkv[0], dkv[1], dw[0], dw[1]

    row_spec = P(('dp', 'cp'))
    in_specs = (row_spec, row_spec, row_spec, row_spec, row_spec, row_spec, P(), P())
    out_specs = (row_spec, row_spec, row_spec, P('dp'), P('dp'))
    return jax.shard_map(local_grads, mesh=mesh, in_specs=in_specs, out_specs=out_specs, check_vma=False)
```

time: 1330 us -> 171 us (0.13); the launches traced: 1320 us -> 171 us
  waiting for transfers between devices: 637 us -> 0 us
  local copies, waits for them, and re-layouts: 317 us -> 6.99 us
  matrix products: 228 us -> 0 us
  Pallas kernels: 0 us -> 153 us
  blocking collectives: 65.6 us -> 0 us
  other arithmetic: 47.6 us -> 9.88 us
  starting transfers between devices: 16.3 us -> 0 us
    ppermute x126 -> x0, waiting for transfers between devices: 637 us -> none  [the longest x31 634 us: visit_source(): v_cur = lax.ppermute(v_cur, 'cp', shift_pairs)]
    dot_general x170 -> x0, matrix products: 228 us -> none  [the longest x34 90.7 us: pair_grads(): jnp.einsum('qngd,knd->qngk', do_blk, v_blk, preferred_element_type=jnp.fl...]
    pallas_call x0 -> x1, Pallas kernels: none -> 153 us  [local_grads(): pl.pallas_call(functools.partial(kernel, side, chunk, per_kv), out_shape=...]
    another operation x60 -> x2, local copies, waits for them, and re-layouts: 152 us -> 0.2 us  [local_grads(): jnp.stack([lse_fwd * LOG2E, delta]).reshape(2, 2, chunk, kv_heads, per_kv)]
    while x127 -> x0, local copies, waits for them, and re-layouts: 105 us -> none
    psum x1 -> x0, blocking collectives: 65.6 us -> none  [local_grads(): lax.psum(dq_weight, 'cp')]
    cond x126 -> x0, local copies, waits for them, and re-layouts: 33.7 us -> none
    ppermute x126 -> x0, starting transfers between devices: 16.3 us -> none  [the longest x31 7.75 us: visit_source(): dv_cur = lax.ppermute(dv_cur, 'cp', shift_pairs)]
  transfers between devices with their start and end apart: 126 -> 0, of which waited for: 35 -> 0; matrix products, arithmetic and copies ran while one was open for 7% -> 0% of each run, Pallas kernels for 0% -> 0%
where the time goes in v1:
time: 171 us
  Pallas kernels  153 us (89%)
  other arithmetic  9.88 us (6%)
  local copies, waits for them, and re-layouts  6.99 us (4%)
    pallas_call x1, Pallas kernels, local_grads(): pl.pallas_call(functools.partial(kernel, side, chunk, per_kv), out_shape=...  153 us
    reduce_sum x1, other arithmetic, local_grads(): delta = jnp.sum(d_out.astype(F32) * out_fwd.astype(F32), axis=-1)  3.43 us

profile of v1, /device:TPU:97, one launch (start us, length us, event | category | flops | bytes accessed | tf_op | source)
XLA Modules:
  0.0 171.1 jit_solution(8447583565694912979)
XLA Ops:
  0.7 0.1 convert_element_type.45
  0.8 0.1 fusion.8
  0.9 0.1 iota_add_fusion
  1.0 0.8 broadcast_multiply_fusion.2
  1.8 0.1 stack.36
  1.9 0.1 broadcast_multiply_fusion.1
  2.0 0.0 copy-start
  2.0 0.0 copy-start.2
  2.0 3.4 %multiply_reduce_fusion = f32[128,64]{1,0:T(8,128)S(1)} fusion(bf16[128,64,128]{2,1,0:T(8,128)(2,1)} %param.11, bf16[128,64,128]{2,1,0:T(8,128)(2,1)} %do_hbm.1), kind=kLoop, calls=%fused_computation | loop fusion | flops 4186112 | bytes 4227072 | tf_op jit(solution)/shard_map/reduce_sum | solution.py:435
  5.4 0.1 copy.48
  5.5 0.0 copy-start.4
  5.5 0.1 stack.37
  5.6 0.1 maximum_bitcast_fusion.1
  5.7 0.0 copy-done
  5.7 0.2 fusion
  6.0 0.1 copy.44
  6.1 0.3 fusion.6
  6.4 0.0 copy-done.2
  6.5 0.2 broadcast_multiply_fusion
  6.7 2.9 %sine_multiply_fusion = (f32[4,2,2,64,128]{4,3,2,1,0:T(8,128)}, f32[4,2,2,64,128]{4,3,2,1,0:T(8,128)}) fusion(f32[4,2,2,64,64]{4,3,2,1,0:T(8,128)S(1)} %broadcast_multiply_fusion, f32[128]{0:T(128)S(1)} %compare_select_fusion), kind=kLoop, calls=%fused_computation.11 | loop fusion | flops 262144 | bytes 1311232 | tf_op jit(solution)/shard_map/mul | solution.py:446
  9.6 0.0 copy-done.4
  9.6 0.2 fusion.1
  9.8 0.2 slice_negate_fusion
  10.0 0.3 fusion.3
  10.4 1.0 maximum_bitcast_fusion.kv_hbm
  11.4 0.4 copy.53
  11.7 1.2 reshape.225.st_hbm
  12.9 153.3 %attention_backward.1 = (bf16[128,64,128]{2,1,0:T(8,128)(2,1)}, bf16[8,2,2,64,128]{4,3,2,1,0:T(8,128)(2,1)}, f32[2,8,128]{2,1,0:T(8,128)}) custom-call(bf16[128,64,128]{2,1,0:T(8,128)(2,1)} %q_hbm.1, bf16[128,64,128]{2,1,0:T(8,128)(2,1)} %do_hbm.1, bf16[8,2,3,64,128]{4,3,2,1,0:T(8,128)(2,1)} %maximum_bitcast_fusion.kv_hbm, f32[8,4,512]{2,1,0:T(4,128)} %reshape.225.st_hbm, ...), custom_call_target="tpu_custom_call" | custom-call | tf_op jit(solution)/shard_map/attention_backward/pallas_call | solution.py:451
  166.2 0.0 copy-start.3
  166.2 0.0 copy-start.1
  166.3 1.2 fusion.10
  167.5 0.9 copy.52
  168.4 0.9 copy.51
  169.2 0.0 copy-done.3
  169.3 0.5 slice_bitcast_fusion
  169.8 0.0 copy-done.1
  169.8 1.3 copy.56
  (12 shorter events, 0.2 us)
Async XLA Ops:
  2.0 3.7 %copy-start = (bf16[128,8,128]{2,1,0:T(8,128)(2,1)S(1)}, bf16[128,8,128]{2,1,0:T(8,128)(2,1)}, u32[]{:S(2)}) copy-start(bf16[128,8,128]{2,1,0:T(8,128)(2,1)} %param.9) | copy-start | bytes 786436
  2.0 4.5 %copy-start.2 = (bf16[128,8,128]{2,1,0:T(8,128)(2,1)S(1)}, bf16[128,8,128]{2,1,0:T(8,128)(2,1)}, u32[]{:S(2)}) copy-start(bf16[128,8,128]{2,1,0:T(8,128)(2,1)} %param.10) | copy-start | bytes 786436
  5.5 4.1 %copy-start.4 = (f32[128]{0:T(128)S(1)}, f32[128]{0:T(128)}, u32[]{:S(2)}) copy-start(f32[128]{0:T(128)} %param.15) | copy-start | bytes 1540
  166.2 3.0 %copy-start.3 = (f32[2,8,128]{2,1,0:T(8,128)S(1)}, f32[2,8,128]{2,1,0:T(8,128)}, u32[]{:S(2)}) copy-start(f32[2,8,128]{2,1,0:T(8,128)} %get-tuple-element.10) | copy-start | bytes 24580
  166.2 3.5 %copy-start.1 = (bf16[128,64,128]{2,1,0:T(8,128)(2,1)S(1)}, bf16[128,64,128]{2,1,0:T(8,128)(2,1)}, u32[]{:S(2)}) copy-start(bf16[128,64,128]{2,1,0:T(8,128)(2,1)} %get-tuple-element.57) | copy-start | bytes 6291460

commit v2 on v1

--- a/solution.py
+++ b/solution.py
@@ -16,7 +16,7 @@
 F32, BF16 = jnp.float32, jnp.bfloat16
 NN = (((1,), (0,)), ((), ()))
 NT = (((1,), (1,)), ((), ()))
-SUB = 16
+SUB = 32
 
 
 def rope_tables(positions):
@@ -40,7 +40,7 @@
 
 def kernel(side, chunk, per_kv, q_hbm, do_hbm, kv_hbm, st_hbm, cos_ref, sin_ref, qn_ref, kn_ref,
            dq_hbm, dkv_hbm, dw_ref,
-           qbuf, dobuf, kbuf, stbuf, q_s, do_s, qT, doT, lc, dc, acc, rsbuf, dq_acc, dqo, dko, dwq, dwk, xbuf,
+           qbuf, dobuf, kbuf, stbuf, q_s, do_s, qT, doT, lc, dc, rb, acc, rsbuf, dq_acc, dqo, dko, dwq, dwk, xbuf,
            in_send, kv_send, kv_recv, st_recv, q_recv, do_recv, ag_send, ag_recv, rs_send, rs_recv,
            dq_send, dq_recv, dk_send, dk_recv, x_send, x_recv):
     me = lax.axis_index('cp')
@@ -52,6 +52,7 @@
     b = (1 - core) * y + core * x
     head = core * side + a
     top = 2 * side - 1
+    local_rows = 2 * chunk
     rows = 2 * chunk * per_kv
     tile = side * 2 * chunk
 
@@ -110,12 +111,19 @@
     sends = []
     for role, ra, slot, d in targets():
         sends.append([remote(s, t, ss, rs, d) for s, t, ss, rs in in_copies(role, ra, slot)])
-    for which in ((0, 1), (2, 3, 4)):
+    def start_own(which):
         for n in which:
             pltpu.make_async_copy(own[n][0], own[n][1], own[n][3]).start()
-        for group in sends:
+
+    def start_sends(groups, which):
+        for group in groups:
             for n in which:
                 group[n].start()
+
+    start_own((0, 1))
+    start_sends(sends, (0, 1))
+    start_own((2, 3, 4))
+    start_sends(sends[:1], (2, 3, 4))
 
     acc[...] = jnp.zeros_like(acc)
     dq_acc[...] = jnp.zeros_like(dq_acc)
@@ -140,6 +148,10 @@
                 cp.start()
                 ag.append(cp)
 
+    for cp in ag:
+        cp.wait_send()
+    start_sends(sends[1:], (2, 3, 4))
+
     def piece_owner(j, i):
         hi = j // side
         jj = j + hi * (top - 2 * j)
@@ -151,8 +163,12 @@
         return cc + lohi * (2 * side * side - 1 - 2 * cc)
 
     def rope_rows(tref, s, cs, lohi, r0):
-        t = tref[s, cs, lohi, pl.ds(r0, SUB), :]
-        return jnp.broadcast_to(t[:, None, :], (SUB, per_kv, HEAD_DIM)).reshape(SUB * per_kv, HEAD_DIM)
+        view = tref.at[s, cs, lohi]
+        return jnp.concatenate([view[pl.ds(r0 + i, per_kv, stride=0), :] for i in range(SUB)], axis=0)
+
+    def stat_rows(n, s, cs, first):
+        t = pltpu.roll(stbuf[s, cs, n], local_rows - first, 1)
+        return jnp.concatenate([jnp.broadcast_to(t[:, i:i + 1], (per_kv, HEAD_DIM)) for i in range(SUB)], axis=0)
 
     def steps(fn):
         n = chunk // SUB
@@ -173,21 +189,25 @@
             dst = pl.ds(pl.multiple_of(t * step_rows, step_rows), step_rows)
             xq = qbuf[s, cs, src].astype(F32).reshape(step_rows, HEAD_DIM)
             ms = jnp.mean(xq * xq, axis=-1, keepdims=True)
-            nq = xq * lax.rsqrt(ms + NORM_EPS) * qn_ref[...]
+            r = jnp.broadcast_to(lax.rsqrt(ms + NORM_EPS), xq.shape)
+            rb[bi, dst, :] = r
+            nq = xq * r * qn_ref[...]
             qf = nq * rope_rows(cos_ref, s, cs, lohi, r0) + pltpu.roll(nq, HEAD_DIM // 2, 1) * rope_rows(sin_ref, s, cs, lohi, r0)
-            q_s[bi, dst, :] = qf.astype(BF16)
-            qT[bi, :, dst] = qf.T.astype(BF16)
+            qf = qf.astype(BF16)
+            q_s[bi, dst, :] = qf
+            qT[bi, :, dst] = qf.T
             dof = dobuf[s, cs, src].astype(F32).reshape(step_rows, HEAD_DIM)
-            do_s[bi, dst, :] = dof.astype(BF16)
-            doT[bi, :, dst] = dof.T.astype(BF16)
-            lanes = pl.ds(pl.multiple_of(sub * step_rows, step_rows), step_rows)
-            lc[bi, dst, :] = jnp.broadcast_to(stbuf[s, cs, pl.ds(lohi, 1), lanes], (HEAD_DIM, step_rows)).T
-            dc[bi, dst, :] = jnp.broadcast_to(stbuf[s, cs, pl.ds(2 + lohi, 1), lanes], (HEAD_DIM, step_rows)).T
+            dof = dof.astype(BF16)
+            do_s[bi, dst, :] = dof
+            doT[bi, :, dst] = dof.T
+            lc[bi, dst, :] = stat_rows(0, s, cs, lohi * chunk + sub * SUB)
+            dc[bi, dst, :] = stat_rows(1, s, cs, lohi * chunk + sub * SUB)
         steps(one)
 
-    def norm_back(g, xr, w, cos_t, sin_t):
-        ms = jnp.mean(xr * xr, axis=-1, keepdims=True)
-        r = lax.rsqrt(ms + NORM_EPS)
+    def inv_rms(xr):
+        return lax.rsqrt(jnp.mean(xr * xr, axis=-1, keepdims=True) + NORM_EPS)
+
+    def norm_back(g, xr, r, w, cos_t, sin_t):
         dn = g * cos_t - pltpu.roll(g, HEAD_DIM // 2, 1) * sin_t
         xh = xr * r
         t = dn * w
@@ -202,9 +222,9 @@
             src = pl.ds(pl.multiple_of(lohi * chunk + sub * SUB, SUB), SUB)
             dst = pl.ds(pl.multiple_of(t * step_rows, step_rows), step_rows)
             xq = qbuf[s, cs, src].astype(F32).reshape(step_rows, HEAD_DIM)
-            dx, dwt = norm_back(dq_acc[bi, dst, :] * SM_SCALE, xq, qn_ref[...],
+            dx, dwt = norm_back(dq_acc[bi, dst, :] * SM_SCALE, xq, rb[bi, dst, :], qn_ref[...],
                                 rope_rows(cos_ref, s, cs, lohi, r0), rope_rows(sin_ref, s, cs, lohi, r0))
-            dwq[...] += jnp.sum(dwt.reshape(SUB, 8, HEAD_DIM) if per_kv == 8 else dwt.reshape(step_rows // 8, 8, HEAD_DIM), axis=0)
+            dwq[...] += jnp.sum(dwt.reshape(step_rows // 8, 8, HEAD_DIM), axis=0)
             dqo[s, cs, src] = dx.reshape(SUB, per_kv, HEAD_DIM).astype(BF16)
         steps(one)
         for cs in range(2):
@@ -250,14 +270,15 @@
     def rs_copy(j, i, lohi, ob, os):
         return remote(acc.at[j, i], rsbuf.at[b, lohi, os], rs_send.at[j, i], rs_recv.at[b, lohi, os], role_dev(core, a, ob))
 
-    n_group = 2
-    per_group = side // n_group
+    n_group = 3
 
     def group_slot(grp, k):
-        n = grp * per_group + k
-        return lax.rem(a + n, side)
+        n = grp + k
+        return lax.rem(a + n + (n // 2) * (side + 1 - 2 * n), side)
 
     def group_body(grp, _):
+        per_group = 1 + grp // 2
+
         def prep_body(k, _):
             s = group_slot(grp, k)
             for cs in range(2):
@@ -324,7 +345,7 @@
             cs = half + lohi * (1 - 2 * half)
             part = slice(half * chunk, (half + 1) * chunk)
             kr = kbuf[jj, ii, half, 2].astype(F32)
-            dx, dwt = norm_back(dk[part], kr, kn_ref[...], cos_ref[s, cs, lohi], sin_ref[s, cs, lohi])
+            dx, dwt = norm_back(dk[part], kr, inv_rms(kr), kn_ref[...], cos_ref[s, cs, lohi], sin_ref[s, cs, lohi])
             dwk[...] += jnp.sum(dwt.reshape(chunk // 8, 8, HEAD_DIM), axis=0)
             dko[lohi, s, half, 0] = dx.astype(BF16)
             dko[lohi, s, half, 1] = dv[part].astype(BF16)
@@ -374,9 +395,6 @@
     for group in sends:
         for cp in group:
             cp.wait_send()
-    for cp in ag:
-        cp.wait_send()
-
     def drain_rs(j, _):
         for i in range(side):
             lohi, ob, os = piece_owner(j, i)
@@ -433,8 +451,8 @@
         k_b = norm_rope(k_raw.astype(F32), k_norm, cos_k[:, None, :], sin_k[:, None, :]).astype(BF16)
         kv = jnp.stack([k_b, v_proj, k_raw]).reshape(3, 2, chunk, kv_heads, HEAD_DIM).transpose(3, 1, 0, 2, 4)
         delta = jnp.sum(d_out.astype(F32) * out_fwd.astype(F32), axis=-1)
-        stats = jnp.stack([lse_fwd * LOG2E, delta]).reshape(2, 2, chunk, kv_heads, per_kv)
-        stats = stats.transpose(3, 0, 1, 2, 4).reshape(kv_heads, 4, chunk * per_kv)
+        stats = jnp.stack([lse_fwd * LOG2E, delta]).reshape(2, local_rows, kv_heads, per_kv)
+        stats = stats.transpose(2, 0, 3, 1)
 
         slots = jnp.arange(side)
         src_chip = jnp.where(core == 0, y * side + slots, slots * side + x)
@@ -459,11 +477,12 @@
                 pltpu.VMEM((side, 2, local_rows, per_kv, HEAD_DIM), BF16),
                 pltpu.VMEM((side, 2, local_rows, per_kv, HEAD_DIM), BF16),
                 pltpu.VMEM((2 * side, side, 2, 3, chunk, HEAD_DIM), BF16),
-                pltpu.VMEM((side, 2, 4, chunk * per_kv), F32),
+                pltpu.VMEM((side, 2, 2, per_kv, local_rows), F32),
                 pltpu.VMEM((2 * side, rows, HEAD_DIM), BF16),
                 pltpu.VMEM((2 * side, rows, HEAD_DIM), BF16),
                 pltpu.VMEM((2 * side, HEAD_DIM, rows), BF16),
                 pltpu.VMEM((2 * side, HEAD_DIM, rows), BF16),
+                pltpu.VMEM((2 * side, rows, HEAD_DIM), F32),
                 pltpu.VMEM((2 * side, rows, HEAD_DIM), F32),
                 pltpu.VMEM((2 * side, rows, HEAD_DIM), F32),
                 pltpu.VMEM((2 * side, side, 2, HEAD_DIM, 2 * chunk), F32),

time: 171 us -> 156 us (0.912)
  Pallas kernels: 153 us -> 139 us
  local copies, waits for them, and re-layouts: 6.99 us -> 5.26 us
    pallas_call x1, Pallas kernels: 153 us -> 139 us  [local_grads(): pl.pallas_call(functools.partial(kernel, side, chunk, per_kv), out_shape=...]
where the time goes in v2:
time: 156 us
  Pallas kernels  139 us (89%)
  other arithmetic  10.5 us (7%)
  local copies, waits for them, and re-layouts  5.26 us (3%)
    pallas_call x1, Pallas kernels, local_grads(): pl.pallas_call(functools.partial(kernel, side, chunk, per_kv), out_shape=...  139 us
    reduce_sum x1, other arithmetic, local_grads(): delta = jnp.sum(d_out.astype(F32) * out_fwd.astype(F32), axis=-1)  3.43 us
    unnamed x15, local copies, waits for them, and re-layouts  3.17 us

profile of v2, /device:TPU:97, one launch (start us, length us, event | category | flops | bytes accessed | tf_op | source)
XLA Modules:
  0.0 155.5 jit_solution(5504008632735705731)
XLA Ops:
  0.7 0.1 convert_element_type.45
  0.8 0.1 fusion.8
  0.9 0.1 iota_add_fusion
  1.0 0.8 multiply_bitcast_fusion
  1.8 0.1 broadcast_multiply_fusion.1
  1.9 0.0 copy-start
  1.9 0.0 copy-start.2
  1.9 3.4 %multiply_reduce_fusion = f32[128,64]{1,0:T(8,128)S(1)} fusion(bf16[128,64,128]{2,1,0:T(8,128)(2,1)} %param.11, bf16[128,64,128]{2,1,0:T(8,128)(2,1)} %do_hbm.1), kind=kLoop, calls=%fused_computation | loop fusion | flops 4186112 | bytes 4227072 | tf_op jit(solution)/shard_map/reduce_sum | solution.py:453
  5.3 0.0 copy-start.4
  5.3 0.1 copy.36
  5.4 0.7 maximum_bitcast_fusion.1.st_hbm
  6.1 0.0 copy-done
  6.1 0.2 fusion
  6.3 0.1 copy.32
  6.5 0.3 fusion.6
  6.8 0.0 copy-done.2
  6.9 0.2 broadcast_multiply_fusion
  7.1 2.9 %sine_multiply_fusion = (f32[4,2,2,64,128]{4,3,2,1,0:T(8,128)}, f32[4,2,2,64,128]{4,3,2,1,0:T(8,128)}) fusion(f32[4,2,2,64,64]{4,3,2,1,0:T(8,128)S(1)} %broadcast_multiply_fusion, f32[128]{0:T(128)S(1)} %compare_select_fusion), kind=kLoop, calls=%fused_computation.11 | loop fusion | flops 262144 | bytes 1311232 | tf_op jit(solution)/shard_map/mul | solution.py:464
  9.9 0.0 copy-done.4
  10.0 0.2 fusion.1
  10.2 0.2 slice_negate_fusion
  10.4 0.3 fusion.3
  10.8 1.0 maximum_bitcast_fusion.kv_hbm
  11.7 139.0 %attention_backward.1 = (bf16[128,64,128]{2,1,0:T(8,128)(2,1)}, bf16[8,2,2,64,128]{4,3,2,1,0:T(8,128)(2,1)}, f32[2,8,128]{2,1,0:T(8,128)}) custom-call(bf16[128,64,128]{2,1,0:T(8,128)(2,1)} %q_hbm.1, bf16[128,64,128]{2,1,0:T(8,128)(2,1)} %do_hbm.1, bf16[8,2,3,64,128]{4,3,2,1,0:T(8,128)(2,1)} %maximum_bitcast_fusion.kv_hbm, ...), custom_call_target="tpu_custom_call" | custom-call | tf_op jit(solution)/shard_map/attention_backward/pallas_call | solution.py:469
  150.7 0.0 copy-start.3
  150.7 0.0 copy-start.1
  150.7 1.2 fusion.10
  151.9 0.9 copy.38
  152.8 0.9 copy.37
  153.7 0.0 copy-done.3
  153.7 0.5 slice_bitcast_fusion
  154.2 0.0 copy-done.1
  154.2 1.3 copy.40
  (12 shorter events, 0.2 us)
Async XLA Ops:
  1.9 4.2 %copy-start = (bf16[128,8,128]{2,1,0:T(8,128)(2,1)S(1)}, bf16[128,8,128]{2,1,0:T(8,128)(2,1)}, u32[]{:S(2)}) copy-start(bf16[128,8,128]{2,1,0:T(8,128)(2,1)} %param.9) | copy-start | bytes 786436
  1.9 4.9 %copy-start.2 = (bf16[128,8,128]{2,1,0:T(8,128)(2,1)S(1)}, bf16[128,8,128]{2,1,0:T(8,128)(2,1)}, u32[]{:S(2)}) copy-start(bf16[128,8,128]{2,1,0:T(8,128)(2,1)} %param.10) | copy-start | bytes 786436
  5.3 4.6 %copy-start.4 = (f32[128]{0:T(128)S(1)}, f32[128]{0:T(128)}, u32[]{:S(2)}) copy-start(f32[128]{0:T(128)} %param.15) | copy-start | bytes 1540
  150.7 3.0 %copy-start.3 = (f32[2,8,128]{2,1,0:T(8,128)S(1)}, f32[2,8,128]{2,1,0:T(8,128)}, u32[]{:S(2)}) copy-start(f32[2,8,128]{2,1,0:T(8,128)} %get-tuple-element.10) | copy-start | bytes 24580
  150.7 3.5 %copy-start.1 = (bf16[128,64,128]{2,1,0:T(8,128)(2,1)S(1)}, bf16[128,64,128]{2,1,0:T(8,128)(2,1)}, u32[]{:S(2)}) copy-start(bf16[128,64,128]{2,1,0:T(8,128)(2,1)} %get-tuple-element.52) | copy-start | bytes 6291460

commit v3 on v2

--- a/solution.py
+++ b/solution.py
@@ -3,6 +3,7 @@
 
 import jax
 import jax.numpy as jnp
+import numpy as np
 from jax import lax
 from jax.experimental import pallas as pl
 from jax.experimental.pallas import tpu as pltpu
@@ -16,30 +17,21 @@
 F32, BF16 = jnp.float32, jnp.bfloat16
 NN = (((1,), (0,)), ((), ()))
 NT = (((1,), (1,)), ((), ()))
-SUB = 32
 
 
 def rope_tables(positions):
-    inv_freq = ROPE_THETA ** (-jnp.arange(0, HEAD_DIM, 2).astype(F32) / HEAD_DIM)
-    angles = positions.astype(F32)[:, None] * inv_freq[None, :]
-    angles = jnp.concatenate([angles, angles], axis=-1)
-    return jnp.cos(angles), jnp.sin(angles)
-
-
-def norm_rope(raw_in, weight, cos_t, sin_t):
-    mean_sq = jnp.mean(raw_in * raw_in, axis=-1, keepdims=True)
-    normed = raw_in * lax.rsqrt(mean_sq + NORM_EPS) * weight
-    half_dim = raw_in.shape[-1] // 2
-    rotated = jnp.concatenate([-normed[..., half_dim:], normed[..., :half_dim]], axis=-1)
-    return normed * cos_t + rotated * sin_t
+    inv_freq = ROPE_THETA ** (-np.arange(0, HEAD_DIM, 2) / HEAD_DIM)
+    angles = np.concatenate([positions[:, None] * inv_freq] * 2, axis=-1)
+    return jnp.asarray(np.cos(angles), F32), jnp.asarray(np.sin(angles), F32)
 
 
 def dot(a, b, dims):
     return lax.dot_general(a, b, dims, preferred_element_type=F32)
 
 
-def kernel(side, chunk, per_kv, q_hbm, do_hbm, kv_hbm, st_hbm, cos_ref, sin_ref, qn_ref, kn_ref,
-           dq_hbm, dkv_hbm, dw_ref,
+def kernel(side, chunk, per_kv, q_hbm, do_hbm, out_hbm, k_ref, v_ref, lse_ref, offc_ref, offs_ref, begc_ref, begs_ref, qn_ref, kn_ref,
+           dq_hbm, dk_ref, dv_ref, dw_ref,
+           cos_ref, sin_ref, do_v, out_v, kv_out, st_out, kst, dk_in, ld_sem,
            qbuf, dobuf, kbuf, stbuf, q_s, do_s, qT, doT, lc, dc, rb, acc, rsbuf, dq_acc, dqo, dko, dwq, dwk, xbuf,
            in_send, kv_send, kv_recv, st_recv, q_recv, do_recv, ag_send, ag_recv, rs_send, rs_recv,
            dq_send, dq_recv, dk_send, dk_recv, x_send, x_recv):
@@ -52,10 +44,20 @@
     b = (1 - core) * y + core * x
     head = core * side + a
     top = 2 * side - 1
+    n_groups = 2 * side
+    SUB = chunk
     local_rows = 2 * chunk
     rows = 2 * chunk * per_kv
     tile = side * 2 * chunk
 
+    n_chunks = 2 * side * side
+
+    def inv_rms(xr):
+        return lax.rsqrt(jnp.mean(xr * xr, axis=-1, keepdims=True) + NORM_EPS)
+
+    def spread(view, width):
+        return jnp.concatenate([view[pl.ds(i, width, stride=0), :] for i in range(chunk)], axis=0)
+
     def role_dev(role, ra, rb):
         return ((1 - role) * (rb * side + ra) + role * (ra * side + rb)) * 2 + role
 
@@ -68,6 +70,10 @@
 
     def landed(ref, sem):
         pltpu.make_async_copy(ref, ref, sem).wait()
+
+    loads = [pltpu.make_async_copy(do_hbm, do_v, ld_sem.at[0]), pltpu.make_async_copy(out_hbm, out_v, ld_sem.at[1])]
+    for cp in loads:
+        cp.start()
 
     barrier = pltpu.get_barrier_semaphore()
     for dx in range(side):
@@ -80,6 +86,30 @@
             else:
                 pl.semaphore_signal(barrier, inc=1, device_id=dev(in_row), device_id_type=pl.DeviceIdType.MESH)
                 pl.semaphore_signal(barrier, inc=1, device_id=dev(in_col), device_id_type=pl.DeviceIdType.MESH)
+
+    def table_body(t, _):
+        s, cs, lohi = t // 4, lax.rem(t // 2, 2), lax.rem(t, 2)
+        src = ((1 - core) * (b * side + s) + core * (s * side + b)) * 2 + cs
+        beg = src + lohi * (2 * n_chunks - 1 - 2 * src)
+        bc, bs = begc_ref[pl.ds(beg, 1), :], begs_ref[pl.ds(beg, 1), :]
+        oc, os = offc_ref[...], offs_ref[...]
+        sign = jnp.where(lax.broadcasted_iota(jnp.int32, oc.shape, 1) < HEAD_DIM // 2, -1.0, 1.0)
+        cos_ref[s, cs, lohi] = bc * oc - bs * os
+        sin_ref[s, cs, lohi] = (bs * oc + bc * os) * sign
+        return 0
+    lax.fori_loop(0, 4 * side, table_body, 0)
+
+    for lohi in range(2):
+        part = slice(lohi * chunk, (lohi + 1) * chunk)
+        kf = k_ref[part].astype(F32).reshape(chunk * n_groups, HEAD_DIM)
+        nk = kf * inv_rms(kf) * kn_ref[...]
+        kb = nk * spread(cos_ref.at[a, core, lohi], n_groups) + pltpu.roll(nk, HEAD_DIM // 2, 1) * spread(sin_ref.at[a, core, lohi], n_groups)
+        vf = v_ref[part].astype(F32).reshape(chunk * n_groups, HEAD_DIM)
+        for n, val in enumerate((kb, vf, kf)):
+            kst[n] = val
+            for h in range(n_groups):
+                kv_out[h, lohi, n] = kst[n, pl.ds(h, chunk, stride=n_groups), :].astype(BF16)
+
     pl.semaphore_wait(barrier, 4 * (side - 1) + 1)
 
     def in_copies(role, ra, slot):
@@ -90,8 +120,8 @@
             jj = y if lohi == 0 else top - y
             ii = x if lohi == 0 else side - 1 - x
             half = core if lohi == 0 else 1 - core
-            kv.append((kv_hbm.at[hd, lohi], kbuf.at[jj, ii, half], kv_send.at[lohi, role, ra], kv_recv.at[lohi, slot, core]))
-        return kv + [(st_hbm.at[hd], stbuf.at[slot, core], in_send.at[0, role, ra], st_recv.at[slot, core]),
+            kv.append((kv_out.at[hd, lohi], kbuf.at[jj, ii, half], kv_send.at[lohi, role, ra], kv_recv.at[lohi, slot, core]))
+        return kv + [(st_out.at[hd], stbuf.at[slot, core], in_send.at[0, role, ra], st_recv.at[slot, core]),
                      (q_hbm.at[:, group, :], qbuf.at[slot, core], in_send.at[1, role, ra], q_recv.at[slot, core]),
                      (do_hbm.at[:, group, :], dobuf.at[slot, core], in_send.at[2, role, ra], do_recv.at[slot, core])]
 
@@ -122,19 +152,39 @@
 
     start_own((0, 1))
     start_sends(sends, (0, 1))
-    start_own((2, 3, 4))
-    start_sends(sends[:1], (2, 3, 4))
+    start_own((3, 4))
+    start_sends(sends[:1], (3, 4))
 
     acc[...] = jnp.zeros_like(acc)
     dq_acc[...] = jnp.zeros_like(dq_acc)
     dwq[...] = jnp.zeros_like(dwq)
     dwk[...] = jnp.zeros_like(dwk)
 
+    for cp in loads:
+        cp.wait()
+    lane = lax.broadcasted_iota(jnp.int32, (n_groups * per_kv, local_rows), 1)
+
+    def delta_body(t, d):
+        for i in range(8):
+            r = t * 8 + i
+            prod = do_v[r].astype(F32) * out_v[r].astype(F32)
+            d = jnp.where(lane == r, jnp.sum(prod, axis=-1, keepdims=True), d)
+        return d
+    delta = lax.fori_loop(0, local_rows // 8, delta_body, jnp.zeros(lane.shape, F32))
+    lse2 = lse_ref[...].T * LOG2E
+    for g in range(n_groups):
+        st_out[g, 0] = lse2[g * per_kv:(g + 1) * per_kv]
+        st_out[g, 1] = delta[g * per_kv:(g + 1) * per_kv]
+    start_own((2,))
+    start_sends(sends, (2,))
+
+    def wanted(lohi, owner, user):
+        return jnp.logical_or(jnp.logical_or(core == 1, lohi == 0), user <= owner)
+
     def place(lohi, s, bb):
         ys, xs = (1 - core) * bb + core * s, (1 - core) * s + core * bb
         return (ys, xs) if lohi == 0 else (top - ys, side - 1 - xs)
 
-    ag = []
     for ds in range(side):
         s = lax.rem(a + ds, side)
         for lohi in range(2):
@@ -143,14 +193,19 @@
                 landed(kbuf.at[jj, ii, cc], kv_recv.at[lohi, s, cc])
             piece = kbuf.at[jj, ii, :, pl.ds(0, 2)]
             for db in range(1, side):
-                cp = remote(piece, piece, ag_send.at[db, lohi, s], ag_recv.at[b, lohi, s],
-                            role_dev(core, a, lax.rem(b + db, side)))
-                cp.start()
-                ag.append(cp)
-
-    for cp in ag:
-        cp.wait_send()
-    start_sends(sends[1:], (2, 3, 4))
+                user = lax.rem(b + db, side)
+
+                @pl.when(wanted(lohi, b, user))
+                def _():
+                    remote(piece, piece, ag_send.at[db, lohi, s], ag_recv.at[b, lohi, s], role_dev(core, a, user)).start()
+
+    for ds in range(side):
+        for lohi in range(2):
+            for db in range(1, side):
+                @pl.when(wanted(lohi, b, lax.rem(b + db, side)))
+                def _():
+                    landed(kbuf.at[0, 0, :, pl.ds(0, 2)], ag_send.at[db, lohi, ds])
+    start_sends(sends[1:], (3, 4))
 
     def piece_owner(j, i):
         hi = j // side
@@ -162,10 +217,6 @@
         cc = (1 - core) * (b * side + s) + core * (s * side + b)
         return cc + lohi * (2 * side * side - 1 - 2 * cc)
 
-    def rope_rows(tref, s, cs, lohi, r0):
-        view = tref.at[s, cs, lohi]
-        return jnp.concatenate([view[pl.ds(r0 + i, per_kv, stride=0), :] for i in range(SUB)], axis=0)
-
     def stat_rows(n, s, cs, first):
         t = pltpu.roll(stbuf[s, cs, n], local_rows - first, 1)
         return jnp.concatenate([jnp.broadcast_to(t[:, i:i + 1], (per_kv, HEAD_DIM)) for i in range(SUB)], axis=0)
@@ -184,7 +235,6 @@
         bi = s * 2 + lohi
 
         def one(t, cs, sub):
-            r0 = pl.multiple_of(sub * SUB, SUB)
             src = pl.ds(pl.multiple_of(lohi * chunk + sub * SUB, SUB), SUB)
             dst = pl.ds(pl.multiple_of(t * step_rows, step_rows), step_rows)
             xq = qbuf[s, cs, src].astype(F32).reshape(step_rows, HEAD_DIM)
@@ -192,7 +242,7 @@
             r = jnp.broadcast_to(lax.rsqrt(ms + NORM_EPS), xq.shape)
             rb[bi, dst, :] = r
             nq = xq * r * qn_ref[...]
-            qf = nq * rope_rows(cos_ref, s, cs, lohi, r0) + pltpu.roll(nq, HEAD_DIM // 2, 1) * rope_rows(sin_ref, s, cs, lohi, r0)
+            qf = nq * spread(cos_ref.at[s, cs, lohi], per_kv) + pltpu.roll(nq, HEAD_DIM // 2, 1) * spread(sin_ref.at[s, cs, lohi], per_kv)
             qf = qf.astype(BF16)
             q_s[bi, dst, :] = qf
             qT[bi, :, dst] = qf.T
@@ -204,9 +254,6 @@
             dc[bi, dst, :] = stat_rows(1, s, cs, lohi * chunk + sub * SUB)
         steps(one)
 
-    def inv_rms(xr):
-        return lax.rsqrt(jnp.mean(xr * xr, axis=-1, keepdims=True) + NORM_EPS)
-
     def norm_back(g, xr, r, w, cos_t, sin_t):
         dn = g * cos_t - pltpu.roll(g, HEAD_DIM // 2, 1) * sin_t
         xh = xr * r
@@ -218,12 +265,11 @@
         bi = s * 2 + lohi
 
         def one(t, cs, sub):
-            r0 = pl.multiple_of(sub * SUB, SUB)
             src = pl.ds(pl.multiple_of(lohi * chunk + sub * SUB, SUB), SUB)
             dst = pl.ds(pl.multiple_of(t * step_rows, step_rows), step_rows)
             xq = qbuf[s, cs, src].astype(F32).reshape(step_rows, HEAD_DIM)
             dx, dwt = norm_back(dq_acc[bi, dst, :] * SM_SCALE, xq, rb[bi, dst, :], qn_ref[...],
-                                rope_rows(cos_ref, s, cs, lohi, r0), rope_rows(sin_ref, s, cs, lohi, r0))
+                                spread(cos_ref.at[s, cs, lohi], per_kv), spread(sin_ref.at[s, cs, lohi], per_kv))
             dwq[...] += jnp.sum(dwt.reshape(step_rows // 8, 8, HEAD_DIM), axis=0)
             dqo[s, cs, src] = dx.reshape(SUB, per_kv, HEAD_DIM).astype(BF16)
         steps(one)
@@ -296,7 +342,7 @@
                 for i in range(side):
                     lohi, ob, os = piece_owner(j, i)
 
-                    @pl.when(ob != b)
+                    @pl.when(jnp.logical_and(ob != b, wanted(lohi, ob, b)))
                     def _():
                         landed(kbuf.at[j, i, :, pl.ds(0, 2)], ag_recv.at[ob, lohi, os])
 
@@ -320,7 +366,7 @@
                 for i in range(side):
                     lohi, ob, os = piece_owner(j, i)
 
-                    @pl.when(ob != b)
+                    @pl.when(jnp.logical_and(ob != b, wanted(lohi, ob, b)))
                     def _():
                         rs_copy(j, i, lohi, ob, os).start()
             return 0
@@ -335,11 +381,12 @@
         ii = xs + lohi * (side - 1 - 2 * xs)
         for db in range(1, side):
             ob = lax.rem(b + db, side)
-            landed(rsbuf.at[ob, lohi, s], rs_recv.at[ob, lohi, s])
+
+            @pl.when(wanted(lohi, b, ob))
+            def _():
+                landed(rsbuf.at[ob, lohi, s], rs_recv.at[ob, lohi, s])
+                acc[jj, ii] += rsbuf[ob, lohi, s]
         total = [acc[jj, ii, n] for n in range(2)]
-        for db in range(1, side):
-            ob = lax.rem(b + db, side)
-            total = [total[n] + rsbuf[ob, lohi, s, n] for n in range(2)]
         dk, dv = total[0].T * SM_SCALE, total[1].T
         for half in range(2):
             cs = half + lohi * (1 - 2 * half)
@@ -350,7 +397,7 @@
             dko[lohi, s, half, 0] = dx.astype(BF16)
             dko[lohi, s, half, 1] = dv[part].astype(BF16)
             target = ((1 - core) * (b * side + s) + core * (s * side + b)) * 2 + cs
-            src, dst = dko.at[lohi, s, half], dkv_hbm.at[head, lohi]
+            src, dst = dko.at[lohi, s, half], dk_in.at[head, lohi]
             mine = target == me
 
             @pl.when(mine)
@@ -363,34 +410,28 @@
         return 0
     lax.fori_loop(0, 2 * side, own_body, 0)
 
-    xbuf[0, a, 0] = dwq[...]
-    xbuf[0, a, 1] = dwk[...]
-    for stage in range(2):
-        pos = (a, b)[stage]
+    mine = x * 2 + core
+    xbuf[0, mine, 0] = dwq[...]
+    xbuf[0, mine, 1] = dwk[...]
+    for stage, (pos, count) in enumerate(((mine, 2 * side), (y, side))):
         cps = []
-        for d in range(1, side):
-            o = lax.rem(pos + d, side)
-            other = role_dev(core, o, b) if stage == 0 else role_dev(core, a, o)
+        for d in range(1, count):
+            o = lax.rem(pos + d, count)
+            other = y * 2 * side + o if stage == 0 else (o * side + x) * 2 + core
             cp = remote(xbuf.at[stage, pos], xbuf.at[stage, pos], x_send.at[stage, d], x_recv.at[stage, pos], other)
             cp.start()
             cps.append(cp)
-        for d in range(1, side):
-            o = lax.rem(pos + d, side)
+        for d in range(1, count):
+            o = lax.rem(pos + d, count)
             landed(xbuf.at[stage, o], x_recv.at[stage, o])
         total = xbuf[stage, 0]
-        for o in range(1, side):
+        for o in range(1, count):
             total = total + xbuf[stage, o]
         for cp in cps:
             cp.wait_send()
         if stage == 0:
-            xbuf[1, b] = total
-        else:
-            xbuf[2, core] = total
-    cp = remote(xbuf.at[2, core], xbuf.at[2, core], x_send.at[2, 0], x_recv.at[2, core], chip * 2 + 1 - core)
-    cp.start()
-    landed(xbuf.at[2, 1 - core], x_recv.at[2, 1 - core])
-    dw_ref[...] = xbuf[2, 0] + xbuf[2, 1]
-    cp.wait_send()
+            xbuf[1, y] = total
+    dw_ref[...] = jnp.sum(total, axis=1)
 
     for group in sends:
         for cp in group:
@@ -399,7 +440,7 @@
         for i in range(side):
             lohi, ob, os = piece_owner(j, i)
 
-            @pl.when(ob != b)
+            @pl.when(jnp.logical_and(ob != b, wanted(lohi, ob, b)))
             def _():
                 rs_copy(j, i, lohi, ob, os).wait_send()
         return 0
@@ -424,9 +465,14 @@
         hd, lohi = t // 2, lax.rem(t, 2)
         part = pl.ds(pl.multiple_of(lohi * chunk, chunk), chunk)
         landed(dq_hbm.at[part, pl.ds(pl.multiple_of(hd * per_kv, per_kv), per_kv), :], dq_recv.at[hd, lohi])
-        landed(dkv_hbm.at[hd, lohi], dk_recv.at[hd, lohi])
+        landed(dk_in.at[hd, lohi], dk_recv.at[hd, lohi])
         return 0
     lax.fori_loop(0, 4 * side, drain_in, 0)
+    for n, ref in enumerate((dk_ref, dv_ref)):
+        for lohi in range(2):
+            for h in range(n_groups):
+                kst[n, pl.ds(h, chunk, stride=n_groups), :] = dk_in[h, lohi, n].astype(F32)
+            ref[lohi * chunk:(lohi + 1) * chunk] = kst[n].reshape(chunk, n_groups, HEAD_DIM).astype(BF16)
 
 
 def solution(mesh):
@@ -434,46 +480,34 @@
     side = math.isqrt(cp_size // 2)
 
     def local_grads(q_raw, k_raw, v_proj, out_fwd, lse_fwd, d_out, q_norm, k_norm):
-        me = lax.axis_index('cp')
         local_rows, num_heads = q_raw.shape[0], q_raw.shape[1]
         chunk = local_rows // 2
         kv_heads = k_raw.shape[1]
         per_kv = num_heads // kv_heads
-        core, chip = me % 2, me // 2
-        x, y = chip % side, chip // side
-
-        offs = jnp.arange(chunk)
-
-        def chunk_positions(device):
-            return jnp.stack([device * chunk + offs, (2 * cp_size - 1 - device) * chunk + offs], axis=-2)
-
-        cos_k, sin_k = rope_tables(chunk_positions(me).reshape(-1))
-        k_b = norm_rope(k_raw.astype(F32), k_norm, cos_k[:, None, :], sin_k[:, None, :]).astype(BF16)
-        kv = jnp.stack([k_b, v_proj, k_raw]).reshape(3, 2, chunk, kv_heads, HEAD_DIM).transpose(3, 1, 0, 2, 4)
-        delta = jnp.sum(d_out.astype(F32) * out_fwd.astype(F32), axis=-1)
-        stats = jnp.stack([lse_fwd * LOG2E, delta]).reshape(2, local_rows, kv_heads, per_kv)
-        stats = stats.transpose(2, 0, 3, 1)
-
-        slots = jnp.arange(side)
-        src_chip = jnp.where(core == 0, y * side + slots, slots * side + x)
-        src_dev = src_chip[:, None] * 2 + jnp.arange(2)[None, :]
-        pos = chunk_positions(src_dev[:, :, None, None])
-        cos_t, sin_t = rope_tables(pos.reshape(-1))
-        sign = jnp.where(jnp.arange(HEAD_DIM) < HEAD_DIM // 2, -1.0, 1.0).astype(F32)
-        cos_t = cos_t.reshape(side, 2, 2, chunk, HEAD_DIM)
-        sin_t = (sin_t * sign).reshape(side, 2, 2, chunk, HEAD_DIM)
+        off_cos, off_sin = rope_tables(np.arange(chunk))
+        beg_cos, beg_sin = rope_tables(np.arange(2 * cp_size) * chunk)
 
         rows = local_rows * per_kv
         dma = pltpu.SemaphoreType.DMA
         any_spec, vmem_spec = pl.BlockSpec(memory_space=pl.ANY), pl.BlockSpec(memory_space=pltpu.VMEM)
-        dq_raw, dkv, dw = pl.pallas_call(
+        return pl.pallas_call(
             functools.partial(kernel, side, chunk, per_kv),
             out_shape=(jax.ShapeDtypeStruct(q_raw.shape, BF16),
-                       jax.ShapeDtypeStruct((kv_heads, 2, 2, chunk, HEAD_DIM), BF16),
-                       jax.ShapeDtypeStruct((2, 8, HEAD_DIM), F32)),
-            in_specs=[any_spec] * 4 + [vmem_spec] * 4,
-            out_specs=(any_spec, any_spec, vmem_spec),
+                       jax.ShapeDtypeStruct(k_raw.shape, BF16),
+                       jax.ShapeDtypeStruct(k_raw.shape, BF16),
+                       jax.ShapeDtypeStruct((2, HEAD_DIM), F32)),
+            in_specs=[any_spec] * 3 + [vmem_spec] * 9,
+            out_specs=(any_spec, vmem_spec, vmem_spec, vmem_spec),
             scratch_shapes=[
+                pltpu.VMEM((side, 2, 2, chunk, HEAD_DIM), F32),
+                pltpu.VMEM((side, 2, 2, chunk, HEAD_DIM), F32),
+                pltpu.VMEM(q_raw.shape, BF16),
+                pltpu.VMEM(q_raw.shape, BF16),
+                pltpu.VMEM((kv_heads, 2, 3, chunk, HEAD_DIM), BF16),
+                pltpu.VMEM((kv_heads, 2, per_kv, local_rows), F32),
+                pltpu.VMEM((3, chunk * kv_heads, HEAD_DIM), F32),
+                pltpu.VMEM((kv_heads, 2, 2, chunk, HEAD_DIM), BF16),
+                dma((2,)),
                 pltpu.VMEM((side, 2, local_rows, per_kv, HEAD_DIM), BF16),
                 pltpu.VMEM((side, 2, local_rows, per_kv, HEAD_DIM), BF16),
                 pltpu.VMEM((2 * side, side, 2, 3, chunk, HEAD_DIM), BF16),
@@ -492,20 +526,21 @@
                 pltpu.VMEM((2, side, 2, 2, chunk, HEAD_DIM), BF16),
                 pltpu.VMEM((8, HEAD_DIM), F32),
                 pltpu.VMEM((8, HEAD_DIM), F32),
-                pltpu.VMEM((3, side, 2, 8, HEAD_DIM), F32),
+                pltpu.VMEM((2, 2 * side, 2, 8, HEAD_DIM), F32),
                 dma((3, 2, side)), dma((2, 2, side)), dma((2, side, 2)), dma((side, 2)), dma((side, 2)), dma((side, 2)),
                 dma((side, 2, side)), dma((side, 2, side)), dma((2 * side, side)), dma((side, 2, side)),
                 dma((side, 2, 2)), dma((kv_heads, 2)), dma((2, side, 2)), dma((kv_heads, 2)),
-                dma((3, side)), dma((3, side)),
+                dma((2, 2 * side)), dma((2, 2 * side)),
             ],
-            compiler_params=pltpu.CompilerParams(collective_id=0, has_side_effects=True, vmem_limit_bytes=60 << 20),
+            compiler_params=pltpu.CompilerParams(collective_id=0, has_side_effects=True, vmem_limit_bytes=63 << 20),
             name='attention_backward',
-        )(q_raw, d_out, kv, stats, cos_t, sin_t, q_norm[None, :], k_norm[None, :])
-        dkv = dkv.transpose(2, 1, 3, 0, 4).reshape(2, local_rows, kv_heads, HEAD_DIM)
-        dw = jnp.sum(dw, axis=1)
-        return dq_raw, dkv[0], dkv[1], dw[0], dw[1]
+        )(q_raw, d_out, out_fwd, k_raw, v_proj, lse_fwd, off_cos, off_sin, beg_cos, beg_sin, q_norm[None, :], k_norm[None, :])
+
+    def grads(*args):
+        dq_raw, dk_raw, dv_proj, dw = local_grads(*args)
+        return dq_raw, dk_raw, dv_proj, dw[0], dw[1]
 
     row_spec = P(('dp', 'cp'))
     in_specs = (row_spec, row_spec, row_spec, row_spec, row_spec, row_spec, P(), P())
     out_specs = (row_spec, row_spec, row_spec, P('dp'), P('dp'))
-    return jax.shard_map(local_grads, mesh=mesh, in_specs=in_specs, out_specs=out_specs, check_vma=False)
+    return jax.shard_map(grads, mesh=mesh, in_specs=in_specs, out_specs=out_specs, check_vma=False)

time: 156 us -> 141 us (0.904)
  other arithmetic: 10.5 us -> 0 us
  Pallas kernels: 139 us -> 133 us
  local copies, waits for them, and re-layouts: 5.26 us -> 7.31 us
    pallas_call x1, Pallas kernels: 139 us -> 133 us  [local_grads(): pl.pallas_call(functools.partial(kernel, side, chunk, per_kv), out_shape=...]
    reduce_sum x3 -> x0, other arithmetic: 3.65 us -> none  [the longest x1 3.43 us: local_grads(): delta = jnp.sum(d_out.astype(F32) * out_fwd.astype(F32), axis=-1)]
    mul x6 -> x0, other arithmetic: 3.42 us -> none  [the longest x1 2.87 us: local_grads(): sin_t = (sin_t * sign).reshape(side, 2, 2, chunk, HEAD_DIM)]
    unnamed x15 -> x8, local copies, waits for them, and re-layouts: 3.17 us -> 6.04 us
    transpose x2 -> x0, other arithmetic: 1.62 us -> none  [the longest x1 0.97 us: local_grads(): jnp.stack([k_b, v_proj, k_raw]).reshape(3, 2, chunk, kv_heads, HEAD_DIM)]
where the time goes in v3:
time: 141 us
  Pallas kernels  133 us (94%)
  local copies, waits for them, and re-layouts  7.31 us (5%)
    pallas_call x1, Pallas kernels, local_grads(): pl.pallas_call(functools.partial(kernel, side, chunk, per_kv), out_shape=...  133 us
    unnamed x8, local copies, waits for them, and re-layouts  6.04 us

profile of v3, /device:TPU:97, one launch (start us, length us, event | category | flops | bytes accessed | tf_op | source)
XLA Modules:
  0.0 140.7 jit_solution(5836073728495322172)
XLA Ops:
  0.6 1.5 %copy.17.lse_ref = f32[128,64]{1,0:T(8,128)} copy(f32[128,64]{0,1:T(8,128)} %param.16) | data formatting | bytes 65536 | tf_op args[4]
  2.1 132.8 %attention_backward.1 = (bf16[128,64,128]{2,1,0:T(8,128)(2,1)}, bf16[128,8,128]{2,1,0:T(8,128)(2,1)}, bf16[128,8,128]{2,1,0:T(8,128)(2,1)}, f32[2,128]{1,0:T(2,128)}) custom-call(bf16[128,64,128]{2,1,0:T(8,128)(2,1)} %q_hbm.1, bf16[128,64,128]{2,1,0:T(8,128)(2,1)} %do_hbm.1, bf16[128,64,128]{2,1,0:T(8,128)(2,1)} %out_hbm.1, bf16[128,8,128]{2,1,0:T(8,128)(2,1)} %k_ref.1, ...), custom_call_target="tpu_custom_call" | custom-call | tf_op jit(solution)/shard_map/attention_backward/pallas_call | solution.py:493
  134.9 1.3 slice_bitcast_fusion
  136.2 0.0 copy-start.1
  136.2 0.0 copy-start
  136.2 3.1 %copy.21 = bf16[128,64,128]{2,1,0:T(8,128)(2,1)} copy(bf16[128,64,128]{2,1,0:T(8,128)(2,1)} %get-tuple-element.20) | data formatting | bytes 4194304
  139.3 0.0 copy-done.1
  139.3 0.7 copy.22
  140.0 0.0 copy-done
  140.0 0.7 copy.23
Async XLA Ops:
  136.2 3.1 %copy-start.1 = (bf16[128,8,128]{2,1,0:T(8,128)(2,1)S(1)}, bf16[128,8,128]{2,1,0:T(8,128)(2,1)}, u32[]{:S(2)}) copy-start(bf16[128,8,128]{2,1,0:T(8,128)(2,1)} %get-tuple-element.21) | copy-start | bytes 786436
  136.2 3.8 %copy-start = (bf16[128,8,128]{2,1,0:T(8,128)(2,1)S(1)}, bf16[128,8,128]{2,1,0:T(8,128)(2,1)}, u32[]{:S(2)}) copy-start(bf16[128,8,128]{2,1,0:T(8,128)(2,1)} %get-tuple-element.22) | copy-start | bytes 786436

commit v4 on v3

--- a/solution.py
+++ b/solution.py
@@ -30,7 +30,7 @@
 
 
 def kernel(side, chunk, per_kv, q_hbm, do_hbm, out_hbm, k_ref, v_ref, lse_ref, offc_ref, offs_ref, begc_ref, begs_ref, qn_ref, kn_ref,
-           dq_hbm, dk_ref, dv_ref, dw_ref,
+           dq_hbm, dk_ref, dv_ref, dwq_ref, dwk_ref,
            cos_ref, sin_ref, do_v, out_v, kv_out, st_out, kst, dk_in, ld_sem,
            qbuf, dobuf, kbuf, stbuf, q_s, do_s, qT, doT, lc, dc, rb, acc, rsbuf, dq_acc, dqo, dko, dwq, dwk, xbuf,
            in_send, kv_send, kv_recv, st_recv, q_recv, do_recv, ag_send, ag_recv, rs_send, rs_recv,
@@ -44,6 +44,7 @@
     b = (1 - core) * y + core * x
     head = core * side + a
     top = 2 * side - 1
+    n_dev = 2 * side * side
     n_groups = 2 * side
     SUB = chunk
     local_rows = 2 * chunk
@@ -76,19 +77,13 @@
         cp.start()
 
     barrier = pltpu.get_barrier_semaphore()
-    for dx in range(side):
-        for cc in range(2):
-            in_row = (y * side + lax.rem(x + dx, side)) * 2 + cc
-            in_col = (lax.rem(y + dx, side) * side + x) * 2 + cc
-            if dx == 0:
-                if cc == 0:
-                    pl.semaphore_signal(barrier, inc=1, device_id=dev(chip * 2 + 1 - core), device_id_type=pl.DeviceIdType.MESH)
-            else:
-                pl.semaphore_signal(barrier, inc=1, device_id=dev(in_row), device_id_type=pl.DeviceIdType.MESH)
-                pl.semaphore_signal(barrier, inc=1, device_id=dev(in_col), device_id_type=pl.DeviceIdType.MESH)
-
-    def table_body(t, _):
-        s, cs, lohi = t // 4, lax.rem(t // 2, 2), lax.rem(t, 2)
+
+    def greet(d, _):
+        pl.semaphore_signal(barrier, inc=1, device_id=dev(lax.rem(me + d, n_dev)), device_id_type=pl.DeviceIdType.MESH)
+        return 0
+    lax.fori_loop(1, n_dev, greet, 0)
+
+    def table(s, cs, lohi):
         src = ((1 - core) * (b * side + s) + core * (s * side + b)) * 2 + cs
         beg = src + lohi * (2 * n_chunks - 1 - 2 * src)
         bc, bs = begc_ref[pl.ds(beg, 1), :], begs_ref[pl.ds(beg, 1), :]
@@ -96,21 +91,14 @@
         sign = jnp.where(lax.broadcasted_iota(jnp.int32, oc.shape, 1) < HEAD_DIM // 2, -1.0, 1.0)
         cos_ref[s, cs, lohi] = bc * oc - bs * os
         sin_ref[s, cs, lohi] = (bs * oc + bc * os) * sign
-        return 0
-    lax.fori_loop(0, 4 * side, table_body, 0)
-
-    for lohi in range(2):
-        part = slice(lohi * chunk, (lohi + 1) * chunk)
-        kf = k_ref[part].astype(F32).reshape(chunk * n_groups, HEAD_DIM)
-        nk = kf * inv_rms(kf) * kn_ref[...]
-        kb = nk * spread(cos_ref.at[a, core, lohi], n_groups) + pltpu.roll(nk, HEAD_DIM // 2, 1) * spread(sin_ref.at[a, core, lohi], n_groups)
-        vf = v_ref[part].astype(F32).reshape(chunk * n_groups, HEAD_DIM)
-        for n, val in enumerate((kb, vf, kf)):
-            kst[n] = val
-            for h in range(n_groups):
-                kv_out[h, lohi, n] = kst[n, pl.ds(h, chunk, stride=n_groups), :].astype(BF16)
-
-    pl.semaphore_wait(barrier, 4 * (side - 1) + 1)
+
+    def table_body(t, _):
+        table(t // 4, lax.rem(t // 2, 2), lax.rem(t, 2))
+        return 0
+
+    table(a, core, 0)
+    table(a, core, 1)
+    pl.semaphore_wait(barrier, n_dev - 1)
 
     def in_copies(role, ra, slot):
         hd = role * side + ra
@@ -132,7 +120,7 @@
         part = 1 - core
         part_a = (1 - part) * x + part * y
         yield part, part_a, part_a, chip * 2 + part
-        for dx in (1, side - 1) + tuple(range(2, side - 1)):
+        for dx in (side - 1, 1) + tuple(range(2, side - 1)):
             for role in range(2):
                 ra = lax.rem(coord(role) + dx, side)
                 yield role, ra, coord(role), role_dev(role, ra, y if role == 0 else x)
@@ -150,10 +138,26 @@
             for n in which:
                 group[n].start()
 
+    near = sends[:5]
+    start_own((3,))
+    start_sends(near[:1], (3,))
+
+    for lohi in range(2):
+        part = slice(lohi * chunk, (lohi + 1) * chunk)
+        kf = k_ref[part].astype(F32).reshape(chunk * n_groups, HEAD_DIM)
+        nk = kf * inv_rms(kf) * kn_ref[...]
+        kb = nk * spread(cos_ref.at[a, core, lohi], n_groups) + pltpu.roll(nk, HEAD_DIM // 2, 1) * spread(sin_ref.at[a, core, lohi], n_groups)
+        vf = v_ref[part].astype(F32).reshape(chunk * n_groups, HEAD_DIM)
+        for n, val in enumerate((kb, vf, kf)):
+            kst[n] = val
+            for h in range(n_groups):
+                kv_out[h, lohi, n] = kst[n, pl.ds(h, chunk, stride=n_groups), :].astype(BF16)
+
     start_own((0, 1))
     start_sends(sends, (0, 1))
-    start_own((3, 4))
-    start_sends(sends[:1], (3, 4))
+    start_own((4,))
+    start_sends(near[:1], (4,))
+    lax.fori_loop(0, 4 * side, table_body, 0)
 
     acc[...] = jnp.zeros_like(acc)
     dq_acc[...] = jnp.zeros_like(dq_acc)
@@ -171,7 +175,7 @@
             d = jnp.where(lane == r, jnp.sum(prod, axis=-1, keepdims=True), d)
         return d
     delta = lax.fori_loop(0, local_rows // 8, delta_body, jnp.zeros(lane.shape, F32))
-    lse2 = lse_ref[...].T * LOG2E
+    lse2 = lse_ref[...] * LOG2E
     for g in range(n_groups):
         st_out[g, 0] = lse2[g * per_kv:(g + 1) * per_kv]
         st_out[g, 1] = delta[g * per_kv:(g + 1) * per_kv]
@@ -185,27 +189,32 @@
         ys, xs = (1 - core) * bb + core * s, (1 - core) * s + core * bb
         return (ys, xs) if lohi == 0 else (top - ys, side - 1 - xs)
 
-    for ds in range(side):
-        s = lax.rem(a + ds, side)
-        for lohi in range(2):
+    for lohi in range(2):
+        for ds in range(side):
+            s = lax.rem(a + ds, side)
             jj, ii = place(lohi, s, b)
             for cc in range(2):
                 landed(kbuf.at[jj, ii, cc], kv_recv.at[lohi, s, cc])
-            piece = kbuf.at[jj, ii, :, pl.ds(0, 2)]
-            for db in range(1, side):
-                user = lax.rem(b + db, side)
-
-                @pl.when(wanted(lohi, b, user))
-                def _():
+        for db in range(side - 1, 0, -1):
+            user = lax.rem(b + db, side)
+
+            @pl.when(wanted(lohi, b, user))
+            def _():
+                for ds in range(side):
+                    s = lax.rem(a + ds, side)
+                    jj, ii = place(lohi, s, b)
+                    piece = kbuf.at[jj, ii, :, pl.ds(0, 2)]
                     remote(piece, piece, ag_send.at[db, lohi, s], ag_recv.at[b, lohi, s], role_dev(core, a, user)).start()
 
-    for ds in range(side):
-        for lohi in range(2):
-            for db in range(1, side):
-                @pl.when(wanted(lohi, b, lax.rem(b + db, side)))
-                def _():
-                    landed(kbuf.at[0, 0, :, pl.ds(0, 2)], ag_send.at[db, lohi, ds])
-    start_sends(sends[1:], (3, 4))
+    def late_sends():
+        for ds in range(side):
+            for lohi in range(2):
+                for db in range(1, side):
+                    @pl.when(wanted(lohi, b, lax.rem(b + db, side)))
+                    def _():
+                        landed(kbuf.at[0, 0, :, pl.ds(0, 2)], ag_send.at[db, lohi, ds])
+        start_sends(near[1:], (3, 4))
+        start_sends(sends[5:], (3, 4))
 
     def piece_owner(j, i):
         hi = j // side
@@ -288,26 +297,27 @@
             def _():
                 remote(src, dst, dq_send.at[s, cs, lohi], dq_recv.at[head, lohi], target).start()
 
-    def compute(s, lohi, j, masked):
+    def compute(s, lohi, j, masked, pieces):
         bi = s * 2 + lohi
-        kt = kbuf[j, :, :, 0].reshape(tile, HEAD_DIM)
-        vt = kbuf[j, :, :, 1].reshape(tile, HEAD_DIM)
-        z = dot(q_s[bi], kt, NT) * (SM_SCALE * LOG2E) - jnp.tile(lc[bi], (1, tile // HEAD_DIM))
+        width = pieces * 2 * chunk
+        kt = kbuf[j, 0:pieces, :, 0].reshape(width, HEAD_DIM)
+        vt = kbuf[j, 0:pieces, :, 1].reshape(width, HEAD_DIM)
+        z = dot(q_s[bi], kt, NT) * (SM_SCALE * LOG2E) - jnp.tile(lc[bi], (1, width // HEAD_DIM))
         if masked:
             first = block_index(s, lohi)
-            row = lax.broadcasted_iota(jnp.int32, (rows, tile), 0) // per_kv
+            row = lax.broadcasted_iota(jnp.int32, (rows, width), 0) // per_kv
             half, off = row // chunk, lax.rem(row, chunk)
             half = half + lohi * (1 - 2 * half)
             q_pos = first * (2 * chunk) + half * chunk + off
-            k_pos = lax.broadcasted_iota(jnp.int32, (rows, tile), 1) + j * tile
+            k_pos = lax.broadcasted_iota(jnp.int32, (rows, width), 1) + j * tile
             z = jnp.where(k_pos <= q_pos, z, -jnp.inf)
         p = jnp.exp2(z)
         dp = dot(do_s[bi], vt, NT)
-        ds = (p * (dp - jnp.tile(dc[bi], (1, tile // HEAD_DIM)))).astype(BF16)
+        ds = (p * (dp - jnp.tile(dc[bi], (1, width // HEAD_DIM)))).astype(BF16)
         pb = p.astype(BF16)
         dv_t = dot(doT[bi], pb, NN)
         dk_t = dot(qT[bi], ds, NN)
-        for i in range(side):
+        for i in range(pieces):
             cols = slice(i * 2 * chunk, (i + 1) * 2 * chunk)
             acc[j, i, 0] += dk_t[:, cols]
             acc[j, i, 1] += dv_t[:, cols]
@@ -317,6 +327,7 @@
         return remote(acc.at[j, i], rsbuf.at[b, lohi, os], rs_send.at[j, i], rs_recv.at[b, lohi, os], role_dev(core, a, ob))
 
     n_group = 3
+    LATE = 3
 
     def group_slot(grp, k):
         n = grp + k
@@ -336,9 +347,17 @@
             return 0
         lax.fori_loop(0, per_group, prep_body, 0)
 
-        def tile_body(j, _):
+        def tile_body(t, _):
+            lohi_t, n = t // side, lax.rem(t, side)
+            o = lax.rem(b + n + grp // 2, side)
+            j = o + lohi_t * (top - 2 * o)
+
             @pl.when(grp == 0)
             def _():
+                @pl.when(t == LATE)
+                def _():
+                    late_sends()
+
                 for i in range(side):
                     lohi, ob, os = piece_owner(j, i)
 
@@ -348,16 +367,20 @@
 
             def block_body(k, _):
                 s, lohi = group_slot(grp, k // 2), lax.rem(k, 2)
-                full = block_index(s, lohi) // side
+                index = block_index(s, lohi)
+                full, wide = index // side, lax.rem(index, side) >= side // 2
 
                 @pl.when(j < full)
                 def _():
-                    compute(s, lohi, j, False)
-
-                @pl.when(j == full)
+                    compute(s, lohi, j, False, side)
+
+                @pl.when(jnp.logical_and(j == full, wide))
                 def _():
-                    compute(s, lohi, j, True)
-                    finish(s, lohi)
+                    compute(s, lohi, j, True, side)
+
+                @pl.when(jnp.logical_and(j == full, jnp.logical_not(wide)))
+                def _():
+                    compute(s, lohi, j, True, side // 2)
                 return 0
             lax.fori_loop(0, 2 * per_group, block_body, 0)
 
@@ -369,6 +392,13 @@
                     @pl.when(jnp.logical_and(ob != b, wanted(lohi, ob, b)))
                     def _():
                         rs_copy(j, i, lohi, ob, os).start()
+
+            @pl.when(n == side - 1)
+            def _():
+                def finish_body(k, _):
+                    finish(group_slot(grp, k), lohi_t)
+                    return 0
+                lax.fori_loop(0, per_group, finish_body, 0)
             return 0
         lax.fori_loop(0, 2 * side, tile_body, 0)
         return 0
@@ -410,28 +440,16 @@
         return 0
     lax.fori_loop(0, 2 * side, own_body, 0)
 
-    mine = x * 2 + core
-    xbuf[0, mine, 0] = dwq[...]
-    xbuf[0, mine, 1] = dwk[...]
-    for stage, (pos, count) in enumerate(((mine, 2 * side), (y, side))):
-        cps = []
-        for d in range(1, count):
-            o = lax.rem(pos + d, count)
-            other = y * 2 * side + o if stage == 0 else (o * side + x) * 2 + core
-            cp = remote(xbuf.at[stage, pos], xbuf.at[stage, pos], x_send.at[stage, d], x_recv.at[stage, pos], other)
-            cp.start()
-            cps.append(cp)
-        for d in range(1, count):
-            o = lax.rem(pos + d, count)
-            landed(xbuf.at[stage, o], x_recv.at[stage, o])
-        total = xbuf[stage, 0]
-        for o in range(1, count):
-            total = total + xbuf[stage, o]
-        for cp in cps:
-            cp.wait_send()
-        if stage == 0:
-            xbuf[1, y] = total
-    dw_ref[...] = jnp.sum(total, axis=1)
+    xbuf[me, 0] = jnp.sum(dwq[...], axis=0, keepdims=True)
+    xbuf[me, 1] = jnp.sum(dwk[...], axis=0, keepdims=True)
+
+    def x_copy(d):
+        return remote(xbuf.at[me], xbuf.at[me], x_send.at[d], x_recv.at[me], lax.rem(me + d, n_dev))
+
+    def x_start(d, _):
+        x_copy(d).start()
+        return 0
+    lax.fori_loop(1, n_dev, x_start, 0)
 
     for group in sends:
         for cp in group:
@@ -468,6 +486,14 @@
         landed(dk_in.at[hd, lohi], dk_recv.at[hd, lohi])
         return 0
     lax.fori_loop(0, 4 * side, drain_in, 0)
+    def x_wait(d, _):
+        x_copy(d).wait_send()
+        o = lax.rem(me + d, n_dev)
+        landed(xbuf.at[o], x_recv.at[o])
+        return 0
+    lax.fori_loop(1, n_dev, x_wait, 0)
+    dwq_ref[...] = jnp.sum(xbuf[:, 0, :, :], axis=0)
+    dwk_ref[...] = jnp.sum(xbuf[:, 1, :, :], axis=0)
     for n, ref in enumerate((dk_ref, dv_ref)):
         for lohi in range(2):
             for h in range(n_groups):
@@ -495,9 +521,10 @@
             out_shape=(jax.ShapeDtypeStruct(q_raw.shape, BF16),
                        jax.ShapeDtypeStruct(k_raw.shape, BF16),
                        jax.ShapeDtypeStruct(k_raw.shape, BF16),
-                       jax.ShapeDtypeStruct((2, HEAD_DIM), F32)),
+                       jax.ShapeDtypeStruct((1, HEAD_DIM), F32),
+                       jax.ShapeDtypeStruct((1, HEAD_DIM), F32)),
             in_specs=[any_spec] * 3 + [vmem_spec] * 9,
-            out_specs=(any_spec, vmem_spec, vmem_spec, vmem_spec),
+            out_specs=(any_spec, vmem_spec, vmem_spec, vmem_spec, vmem_spec),
             scratch_shapes=[
                 pltpu.VMEM((side, 2, 2, chunk, HEAD_DIM), F32),
                 pltpu.VMEM((side, 2, 2, chunk, HEAD_DIM), F32),
@@ -526,19 +553,19 @@
                 pltpu.VMEM((2, side, 2, 2, chunk, HEAD_DIM), BF16),
                 pltpu.VMEM((8, HEAD_DIM), F32),
                 pltpu.VMEM((8, HEAD_DIM), F32),
-                pltpu.VMEM((2, 2 * side, 2, 8, HEAD_DIM), F32),
+                pltpu.VMEM((cp_size, 2, 1, HEAD_DIM), F32),
                 dma((3, 2, side)), dma((2, 2, side)), dma((2, side, 2)), dma((side, 2)), dma((side, 2)), dma((side, 2)),
                 dma((side, 2, side)), dma((side, 2, side)), dma((2 * side, side)), dma((side, 2, side)),
                 dma((side, 2, 2)), dma((kv_heads, 2)), dma((2, side, 2)), dma((kv_heads, 2)),
-                dma((2, 2 * side)), dma((2, 2 * side)),
+                dma((cp_size,)), dma((cp_size,)),
             ],
             compiler_params=pltpu.CompilerParams(collective_id=0, has_side_effects=True, vmem_limit_bytes=63 << 20),
             name='attention_backward',
-        )(q_raw, d_out, out_fwd, k_raw, v_proj, lse_fwd, off_cos, off_sin, beg_cos, beg_sin, q_norm[None, :], k_norm[None, :])
+        )(q_raw, d_out, out_fwd, k_raw, v_proj, lse_fwd.T, off_cos, off_sin, beg_cos, beg_sin, q_norm[None, :], k_norm[None, :])
 
     def grads(*args):
-        dq_raw, dk_raw, dv_proj, dw = local_grads(*args)
-        return dq_raw, dk_raw, dv_proj, dw[0], dw[1]
+        dq_raw, dk_raw, dv_proj, dq_norm, dk_norm = local_grads(*args)
+        return dq_raw, dk_raw, dv_proj, dq_norm[0], dk_norm[0]
 
     row_spec = P(('dp', 'cp'))
     in_specs = (row_spec, row_spec, row_spec, row_spec, row_spec, row_spec, P(), P())

time: 141 us -> 129 us (0.915)
  Pallas kernels: 133 us -> 123 us
  local copies, waits for them, and re-layouts: 7.31 us -> 5.58 us
    pallas_call x1, Pallas kernels: 133 us -> 123 us  [local_grads(): pl.pallas_call(functools.partial(kernel, side, chunk, per_kv), out_shape=...]
    unnamed x8 -> x13, local copies, waits for them, and re-layouts: 6.04 us -> 5.58 us
where the time goes in v4:
time: 129 us
  Pallas kernels  123 us (95%)
  local copies, waits for them, and re-layouts  5.58 us (4%)
    pallas_call x1, Pallas kernels, local_grads(): pl.pallas_call(functools.partial(kernel, side, chunk, per_kv), out_shape=...  123 us
    unnamed x13, local copies, waits for them, and re-layouts  5.58 us

profile of v4, /device:TPU:97, one launch (start us, length us, event | category | flops | bytes accessed | tf_op | source)
XLA Modules:
  0.0 129.1 jit_solution(5213652472036447376)
XLA Ops:
  0.6 122.9 %attention_backward.1 = (bf16[128,64,128]{2,1,0:T(8,128)(2,1)}, bf16[128,8,128]{2,1,0:T(8,128)(2,1)}, bf16[128,8,128]{2,1,0:T(8,128)(2,1)}, f32[1,128]{1,0:T(1,128)}, f32[1,128]{1,0:T(1,128)}) custom-call(bf16[128,64,128]{2,1,0:T(8,128)(2,1)} %q_hbm.1, bf16[128,64,128]{2,1,0:T(8,128)(2,1)} %do_hbm.1, bf16[128,64,128]{2,1,0:T(8,128)(2,1)} %out_hbm.1, ...), custom_call_target="tpu_custom_call" | custom-call | tf_op jit(solution)/shard_map/attention_backward/pallas_call | solution.py:519
  123.5 0.0 copy-start.1
  123.5 0.0 copy-start
  123.5 0.0 copy-start.3
  123.5 0.0 copy-start.2
  123.5 3.1 %copy.22 = bf16[128,64,128]{2,1,0:T(8,128)(2,1)} copy(bf16[128,64,128]{2,1,0:T(8,128)(2,1)} %get-tuple-element.20) | data formatting | bytes 4194304
  126.7 0.0 copy-done.1
  126.7 0.7 copy.23
  127.4 0.0 copy-done
  127.4 0.7 copy.24
  128.1 0.0 copy-done.3
  128.1 0.5 copy.25
  128.6 0.0 copy-done.2
  128.6 0.5 copy.26
Async XLA Ops:
  123.5 3.2 %copy-start.1 = (bf16[128,8,128]{2,1,0:T(8,128)(2,1)S(1)}, bf16[128,8,128]{2,1,0:T(8,128)(2,1)}, u32[]{:S(2)}) copy-start(bf16[128,8,128]{2,1,0:T(8,128)(2,1)} %get-tuple-element.21) | copy-start | bytes 786436
  123.5 3.9 %copy-start = (bf16[128,8,128]{2,1,0:T(8,128)(2,1)S(1)}, bf16[128,8,128]{2,1,0:T(8,128)(2,1)}, u32[]{:S(2)}) copy-start(bf16[128,8,128]{2,1,0:T(8,128)(2,1)} %get-tuple-element.22) | copy-start | bytes 786436
  123.5 4.6 %copy-start.3 = (f32[1,128]{1,0:T(1,128)S(1)}, f32[1,128]{1,0:T(1,128)}, u32[]{:S(2)}) copy-start(f32[1,128]{1,0:T(1,128)} %get-tuple-element.13) | copy-start | bytes 1540
  123.5 5.1 %copy-start.2 = (f32[1,128]{1,0:T(1,128)S(1)}, f32[1,128]{1,0:T(1,128)}, u32[]{:S(2)}) copy-start(f32[1,128]{1,0:T(1,128)} %get-tuple-element.14) | copy-start | bytes 1540

commit v5 on v4

--- a/solution.py
+++ b/solution.py
@@ -140,7 +140,7 @@
 
     near = sends[:5]
     start_own((3,))
-    start_sends(near[:1], (3,))
+    start_sends(near, (3,))
 
     for lohi in range(2):
         part = slice(lohi * chunk, (lohi + 1) * chunk)
@@ -156,7 +156,7 @@
     start_own((0, 1))
     start_sends(sends, (0, 1))
     start_own((4,))
-    start_sends(near[:1], (4,))
+    start_sends(near, (4,))
     lax.fori_loop(0, 4 * side, table_body, 0)
 
     acc[...] = jnp.zeros_like(acc)
@@ -213,7 +213,6 @@
                     @pl.when(wanted(lohi, b, lax.rem(b + db, side)))
                     def _():
                         landed(kbuf.at[0, 0, :, pl.ds(0, 2)], ag_send.at[db, lohi, ds])
-        start_sends(near[1:], (3, 4))
         start_sends(sends[5:], (3, 4))
 
     def piece_owner(j, i):
@@ -331,7 +330,7 @@
 
     def group_slot(grp, k):
         n = grp + k
-        return lax.rem(a + n + (n // 2) * (side + 1 - 2 * n), side)
+        return lax.rem(a + lax.rem(2 * n + 1, side + 1), side)
 
     def group_body(grp, _):
         per_group = 1 + grp // 2

time: 129 us -> 127 us (0.984)
  Pallas kernels: 123 us -> 121 us
    pallas_call x1, Pallas kernels: 123 us -> 121 us  [local_grads(): pl.pallas_call(functools.partial(kernel, side, chunk, per_kv), out_shape=...]
where the time goes in v5:
time: 127 us
  Pallas kernels  121 us (95%)
  local copies, waits for them, and re-layouts  5.58 us (4%)
    pallas_call x1, Pallas kernels, local_grads(): pl.pallas_call(functools.partial(kernel, side, chunk, per_kv), out_shape=...  121 us
    unnamed x13, local copies, waits for them, and re-layouts  5.58 us

profile of v5, /device:TPU:97, one launch (start us, length us, event | category | flops | bytes accessed | tf_op | source)
XLA Modules:
  0.0 127.2 jit_solution(17643990400436876798)
XLA Ops:
  0.6 121.0 %attention_backward.1 = (bf16[128,64,128]{2,1,0:T(8,128)(2,1)}, bf16[128,8,128]{2,1,0:T(8,128)(2,1)}, bf16[128,8,128]{2,1,0:T(8,128)(2,1)}, f32[1,128]{1,0:T(1,128)}, f32[1,128]{1,0:T(1,128)}) custom-call(bf16[128,64,128]{2,1,0:T(8,128)(2,1)} %q_hbm.1, bf16[128,64,128]{2,1,0:T(8,128)(2,1)} %do_hbm.1, bf16[128,64,128]{2,1,0:T(8,128)(2,1)} %out_hbm.1, ...), custom_call_target="tpu_custom_call" | custom-call | tf_op jit(solution)/shard_map/attention_backward/pallas_call | solution.py:518
  121.6 0.0 copy-start.1
  121.6 0.0 copy-start
  121.6 0.0 copy-start.3
  121.7 0.0 copy-start.2
  121.7 3.1 %copy.22 = bf16[128,64,128]{2,1,0:T(8,128)(2,1)} copy(bf16[128,64,128]{2,1,0:T(8,128)(2,1)} %get-tuple-element.20) | data formatting | bytes 4194304
  124.8 0.0 copy-done.1
  124.8 0.7 copy.23
  125.5 0.0 copy-done
  125.5 0.7 copy.24
  126.2 0.0 copy-done.3
  126.2 0.5 copy.25
  126.7 0.0 copy-done.2
  126.7 0.5 copy.26
Async XLA Ops:
  121.6 3.2 %copy-start.1 = (bf16[128,8,128]{2,1,0:T(8,128)(2,1)S(1)}, bf16[128,8,128]{2,1,0:T(8,128)(2,1)}, u32[]{:S(2)}) copy-start(bf16[128,8,128]{2,1,0:T(8,128)(2,1)} %get-tuple-element.21) | copy-start | bytes 786436
  121.6 3.9 %copy-start = (bf16[128,8,128]{2,1,0:T(8,128)(2,1)S(1)}, bf16[128,8,128]{2,1,0:T(8,128)(2,1)}, u32[]{:S(2)}) copy-start(bf16[128,8,128]{2,1,0:T(8,128)(2,1)} %get-tuple-element.22) | copy-start | bytes 786436
  121.6 4.6 %copy-start.3 = (f32[1,128]{1,0:T(1,128)S(1)}, f32[1,128]{1,0:T(1,128)}, u32[]{:S(2)}) copy-start(f32[1,128]{1,0:T(1,128)} %get-tuple-element.13) | copy-start | bytes 1540
  121.7 5.1 %copy-start.2 = (f32[1,128]{1,0:T(1,128)S(1)}, f32[1,128]{1,0:T(1,128)}, u32[]{:S(2)}) copy-start(f32[1,128]{1,0:T(1,128)} %get-tuple-element.14) | copy-start | bytes 1540
